TPU v7x, 32 devices: a whole 2x2x4 slice. The times are simulated.
32 devices in a mesh: cp: 32 (over z, y, x, core).
Axes of the slice: x: 2, y: 2, z: 4, core: 2. Of those that a mesh axis runs over, the one named last changes fastest.
Arguments:
- x_seq: bfloat16 [1, 24576, 80, 64], P(None, 'cp')
- dt_seq: float32 [1, 24576, 80], P(None, 'cp')
- a_log: float32 [80], replicated
- b_proj: bfloat16 [1, 24576, 128], P(None, 'cp')
- c_proj: bfloat16 [1, 24576, 128], P(None, 'cp')
- d_skip: float32 [80], replicated
- s_init: float32 [1, 80, 64, 128], replicated
- dy_seq: bfloat16 [1, 24576, 80, 64], P(None, 'cp')
- ds_last: float32 [1, 80, 64, 128], replicated
Outputs:
- output 1: bfloat16 [1, 24576, 80, 64], P(None, 'cp')
- output 2: float32 [1, 24576, 80], P(None, 'cp')
- output 3: bfloat16 [1, 24576, 128], P(None, 'cp')
- output 4: bfloat16 [1, 24576, 128], P(None, 'cp')
- output 5: float32 [1, 80, 64, 128], replicated
- output 6: float32 [80], replicated
- output 7: float32 [80], replicated
All inputs are finite; a program needn't handle non-finite values.
Results may differ from a plain program's by a relative error of at most 0.001.
Values sent between devices are 32-bit elements.
A program may use at most 1 GiB of HBM per device.

v0:
```python
import functools
import jax
import jax.numpy as jnp
from jax import lax
from jax.sharding import PartitionSpec as P, NamedSharding

CHUNK = 256
AXIS = 'cp'
HIGH_PREC = lax.Precision.HIGHEST


def chunk_step(carry_state, blk_in, neg_rate, d_skip):
    x_blk, dt_blk, b_blk, c_blk = blk_in
    cum_decay = jnp.cumsum(dt_blk * neg_rate, axis=1)
    u_blk = x_blk * dt_blk[..., None]
    gram_mat = jnp.einsum('btn,bsn->bts', c_blk, b_blk, precision=HIGH_PREC, preferred_element_type=jnp.float32)
    blk_len = x_blk.shape[1]
    causal = (jnp.arange(blk_len)[:, None] >= jnp.arange(blk_len)[None, :])[None, :, :, None]
    log_diff = jnp.where(causal, cum_decay[:, :, None, :] - cum_decay[:, None, :, :], 0.0)
    mix_mat = jnp.where(causal, jnp.exp(log_diff), 0.0) * gram_mat[..., None]
    y_blk = jnp.einsum('btsh,bshp->bthp', mix_mat, u_blk, precision=HIGH_PREC, preferred_element_type=jnp.float32)
    y_blk = y_blk + jnp.exp(cum_decay)[..., None] * jnp.einsum('bhpn,btn->bthp', carry_state, c_blk, precision=HIGH_PREC, preferred_element_type=jnp.float32)
    y_blk = y_blk + d_skip[:, None] * x_blk
    tail_decay = jnp.exp(cum_decay[:, -1:, :] - cum_decay)
    new_state = jnp.exp(cum_decay[:, -1, :])[..., None, None] * carry_state + jnp.einsum('bsh,bshp,bsn->bhpn', tail_decay, u_blk, b_blk, precision=HIGH_PREC, preferred_element_type=jnp.float32)
    return new_state, y_blk


def ssd_forward(x_seq, dt_seq, a_log, b_proj, c_proj, d_skip, s_init, n_span):
    n_batch, seq_len = x_seq.shape[0], x_seq.shape[1]
    per_span = seq_len // (n_span * CHUNK)
    neg_rate = -jnp.exp(a_log)
    inner_step = jax.checkpoint(functools.partial(chunk_step, neg_rate=neg_rate, d_skip=d_skip))

    def span_step(carry_state, span_in):
        return lax.scan(inner_step, carry_state, span_in)

    def split_seq(array_in):
        blocks = array_in.astype(jnp.float32).reshape((n_batch, n_span, per_span, CHUNK) + array_in.shape[2:])
        return jnp.moveaxis(blocks, 0, 2)

    seq_in = (split_seq(x_seq), split_seq(dt_seq), split_seq(b_proj), split_seq(c_proj))
    final_state, y_blocks = lax.scan(jax.checkpoint(span_step), s_init, seq_in)
    y_seq = jnp.moveaxis(y_blocks, 2, 0).reshape(x_seq.shape)
    return y_seq, final_state


def shard_summary(x_loc, dt_loc, a_log, b_loc, c_loc, dy_loc):
    cum_decay = jnp.cumsum(dt_loc * (-jnp.exp(a_log)), axis=1)
    log_total = cum_decay[:, -1, :]
    in_weight = jnp.exp(log_total[:, None, :] - cum_decay) * dt_loc
    x_weighted = x_loc.astype(jnp.float32) * in_weight[..., None]
    state_part = jnp.einsum('bthp,btn->bhpn', x_weighted, b_loc.astype(jnp.float32), precision=HIGH_PREC, preferred_element_type=jnp.float32)
    dy_weighted = dy_loc.astype(jnp.float32) * jnp.exp(cum_decay)[..., None]
    grad_part = jnp.einsum('bthp,btn->bhpn', dy_weighted, c_loc.astype(jnp.float32), precision=HIGH_PREC, preferred_element_type=jnp.float32)
    return state_part, grad_part, log_total


def link_states(state_all, grad_all, logdec_all, dev_idx, s_init, ds_last):
    log_before = jnp.cumsum(logdec_all, axis=0) - logdec_all
    log_total = jnp.sum(logdec_all, axis=0)
    log_here = log_before[dev_idx]
    log_after = log_here + logdec_all[dev_idx]
    dev_order = jnp.arange(logdec_all.shape[0])[:, None, None]
    w_left = jnp.where(dev_order < dev_idx, jnp.exp(jnp.minimum(log_here[None] - log_before - logdec_all, 0.0)), 0.0)
    s_start = jnp.exp(log_here)[..., None, None] * s_init + jnp.einsum('jbh,jbhpn->bhpn', w_left, state_all, precision=HIGH_PREC, preferred_element_type=jnp.float32)
    w_right = jnp.where(dev_order > dev_idx, jnp.exp(jnp.minimum(log_before - log_after[None], 0.0)), 0.0)
    ds_end = jnp.exp(log_total - log_after)[..., None, None] * ds_last + jnp.einsum('jbh,jbhpn->bhpn', w_right, grad_all, precision=HIGH_PREC, preferred_element_type=jnp.float32)
    ds_first = jnp.exp(log_total)[..., None, None] * ds_last + jnp.einsum('jbh,jbhpn->bhpn', jnp.exp(log_before), grad_all, precision=HIGH_PREC, preferred_element_type=jnp.float32)
    return s_start, ds_end, ds_first


def solution(mesh):
    tok4 = P(None, AXIS, None, None)
    tok3 = P(None, AXIS, None)

    def device_step(x_loc, dt_loc, a_log, b_loc, c_loc, d_skip, s_init, dy_loc, ds_last):
        dev_idx = lax.axis_index(AXIS)
        state_part, grad_part, log_part = shard_summary(x_loc, dt_loc, a_log, b_loc, c_loc, dy_loc)
        state_all = lax.all_gather(state_part, AXIS)
        grad_all = lax.all_gather(grad_part, AXIS)
        logdec_all = lax.all_gather(log_part, AXIS)
        s_start, ds_end, ds_first = link_states(state_all, grad_all, logdec_all, dev_idx, s_init, ds_last)

        def local_forward(x_in, dt_in, alog_in, b_in, c_in, skip_in):
            return ssd_forward(x_in, dt_in, alog_in, b_in, c_in, skip_in, s_start, 1)

        _, pull_back = jax.vjp(local_forward, x_loc, dt_loc, a_log, b_loc, c_loc, d_skip)
        grad_x, grad_dt, grad_alog, grad_b, grad_c, grad_skip = pull_back((dy_loc.astype(jnp.float32), ds_end))
        grad_alog, grad_skip = lax.psum((grad_alog, grad_skip), AXIS)
        return grad_x, grad_dt, grad_b, grad_c, ds_first, grad_alog, grad_skip

    return jax.shard_map(device_step, mesh=mesh,
                         in_specs=(tok4, tok3, P(), tok3, tok3, P(), P(), tok4, P()),
                         out_specs=(tok4, tok3, tok3, tok3, P(), P(), P()),
                         check_vma=False)
```

profile of v0, /device:TPU:0, one launch (start us, length us, event | category | flops | bytes accessed | tf_op | source)
XLA Modules:
  0.0 1517.9 jit_solution(3773133234275138697)
XLA Ops:
  11.5 11.4 fusion.105
  23.3 11.4 fusion.107
  34.8 22.9 %squeeze.118 = f32[3,1,256,80,64]{2,0,4,3,1:T(4,128)} reshape(bf16[1,768,80,64]{1,3,2,0:T(8,128)(2,1)} %param.13) | data formatting | bytes 23592960 | tf_op jit(solution)/shard_map/transpose(jvp())/while/body/jit(dynamic_index_in_dim)/squeeze | solution.py:43
  57.7 22.9 %squeeze.125 = f32[3,1,256,80,64]{2,0,4,3,1:T(4,128)} reshape(bf16[1,768,80,64]{1,3,2,0:T(8,128)(2,1)} %param.20) | data formatting | bytes 23592960 | tf_op jit(solution)/shard_map/transpose(jvp())/while/body/jit(dynamic_index_in_dim)/squeeze | solution.py:43
  81.5 43.5 %all_gather.15 = f32[32,1,80]{2,1,0:T(1,128)S(1)} all-gather(f32[1,1,80]{2,1,0:T(1,128)S(1)} %copy.179), channel_id=1, replica_groups=mesh['cp'=32] {'cp'}, dimensions={0}, use_global_device_ids=true | all-gather | bytes 10560 | tf_op jit(solution)/shard_map/all_gather | solution.py:82
  126.5 335.0 %all-gather.7.cloned.1.call-done = f32[2560,64,128]{2,1,0:T(8,128)} async-done(((f32[80,64,128]{2,1,0:T(8,128)}), f32[2560,64,128]{2,1,0:T(8,128)}) %all-gather.7.cloned.1.call-update) | async-done | bytes 83886096 | tf_op jit(solution)/shard_map/all_gather | solution.py:81
  461.5 105.8 %fusion.103 = f32[80,1,64,128]{3,1,2,0:T(1,128)} fusion(f32[32,80,1,1]{0,2,3,1:T(1,128)S(1)} %copy.197, f32[32,80,64,128]{3,2,1,0:T(8,128)} %bitcast.37), kind=kOutput, calls=%fused_computation.134 | convolution fusion | flops 251658240 | bytes 86517760 | tf_op jit(solution)/shard_map/jbh,jbhpn->bhpn/dot_general | solution.py:68
  567.3 105.6 %fusion.101 = f32[80,1,64,128]{3,1,2,0:T(1,128)} fusion(f32[32,80,1,1]{0,2,3,1:T(1,128)S(1)} %copy.200, f32[32,80,64,128]{3,2,1,0:T(8,128)} %bitcast.37), kind=kOutput, calls=%fused_computation.132 | convolution fusion | flops 251658240 | bytes 86517760 | tf_op jit(solution)/shard_map/jbh,jbhpn->bhpn/dot_general | solution.py:69
  672.9 225.9 %all-gather.5.cloned.1.call-done = f32[2560,64,128]{2,1,0:T(8,128)} async-done(((f32[80,64,128]{2,1,0:T(8,128)}), f32[2560,64,128]{2,1,0:T(8,128)}) %all-gather.5.cloned.1.call-update) | async-done | bytes 83886096 | tf_op jit(solution)/shard_map/all_gather | solution.py:80
  898.8 103.6 %fusion.99 = f32[80,1,64,128]{3,1,2,0:T(1,128)S(1)} fusion(f32[32,80,1,1]{0,2,3,1:T(1,128)S(1)} %copy.194, f32[32,80,64,128]{3,2,1,0:T(8,128)} %bitcast.23), kind=kOutput, calls=%fused_computation.130 | convolution fusion | flops 251658240 | bytes 86517760 | tf_op jit(solution)/shard_map/jbh,jbhpn->bhpn/dot_general | solution.py:66
  1008.5 14.3 copy.180
  1022.8 35.2 %while.73 = (s32[]{:T(128)}, f32[1,80,64,128]{3,2,1,0:T(8,128)S(1)}, f32[3,1,80,64,128]{4,3,2,1,0:T(8,128)}, f32[3,1,256,80]{2,0,3,1:T(4,128)}, f32[1,1,80]{2,1,...) while((s32[]{:T(128)}, ...), condition=%wide.region_7.8_spmd, body=%wide.region_4.7_spmd.sunk | while | flops 2019860736 | bytes 17590184 | solution.py:36
  1028.3 6.2 bitcast_add_fusion.12
  1040.1 6.2 bitcast_add_fusion.12
  1051.9 6.2 bitcast_add_fusion.12
  1058.1 4.1 broadcast.318
  1063.7 399.6 %while.74 = (s32[]{:T(128)}, f32[80]{0:T(128)S(1)}, f32[80]{0:T(128)S(1)}, f32[1,80,64,128]{3,2,1,0:T(8,128)}, bf16[3,1,256,80,64]{2,4,3,1,0:T(8,128)(2,1)}, /*i...) while((s32[]{:T(128)}, f32[80]{0:T(128)S(1)}, ...), condition=%wide.region_22.23_spmd.clone, body=%wide.region_8.22_spmd.clone.sunk | while | flops 18533126144 | bytes 189499920 | solution.py:36
  1063.9 9.1 constant_dynamic-slice_fusion.6
  1073.0 7.6 copy_bitcast_fusion.6
  1081.5 3.5 dynamic-slice_bitcast_fusion.8
  1087.4 11.4 fusion.185
  1099.4 32.8 %fusion.178 = (f32[256,80]{0,1:T(8,128)S(1)}, f32[256,80]{0,1:T(8,128)S(1)}, f32[256,256]{1,0:T(8,128)S(1)}) fusion(f32[256,80]{0,1:T(8,128)S(1)} %copy.259, f32[256,256]{1,0:T(8,128)S(1)} %fusion.175, pred[256,256]{1,0:T(8,128)(4,1)S(1)} %iota_compare_fusion.4, f32[1,256,80,64]{1,3,2,0:T(8,128)} %get-tuple-element.928, ...), kind=kOutput, calls=%fused_computation.34.clone.1 | convolution fusion | flops 4085407744 | bytes 11403264 | tf_op jit(solution)/shard_map/transpose(jvp())/while/body/eval_jaxpr/checkpoint/while/body/eval_jaxpr/checkpoint/btsh,bshp->bthp/dot_general | solution.py:21
  1132.6 8.4 fusion.176
  1144.6 21.9 %multiply_reduce_fusion.6 = (f32[256,80]{0,1:T(8,128)S(1)}, f32[80]{0:T(128)S(1)}, f32[1,256,80,64]{1,3,2,0:T(8,128)S(1)}) fusion(f32[1,256,80,64]{1,3,2,0:T(8,128)} %get-tuple-element.928, f32[1,256,80,64]{1,3,2,0:T(8,128)} %get-tuple-element.929, f32[256,256]{1,0:T(8,128)S(1)} %fusion.175, f32[256,80]{0,1:T(8,128)S(1)} %copy.259, ...), kind=kOutput, calls=%fused_computation.58.clone.1 | convolution fusion | flops 4055347200 | bytes 21545280 | tf_op jit(solution)/shard_map/transpose(jvp())/while/body/eval_jaxpr/checkpoint/while/body/eval_jaxpr/checkpoint/btsh,bshp->bthp/dot_general | solution.py:21
  1169.3 8.0 fusion.184
  1177.3 7.1 bitcast_add_fusion.14
  1184.3 4.5 fusion.179
  1196.4 9.1 constant_dynamic-slice_fusion.6
  1205.5 7.6 copy_bitcast_fusion.6
  1220.0 11.4 fusion.185
  1231.9 32.7 %fusion.178 = (f32[256,80]{0,1:T(8,128)S(1)}, f32[256,80]{0,1:T(8,128)S(1)}, f32[256,256]{1,0:T(8,128)S(1)}) fusion(f32[256,80]{0,1:T(8,128)S(1)} %copy.259, f32[256,256]{1,0:T(8,128)S(1)} %fusion.175, pred[256,256]{1,0:T(8,128)(4,1)S(1)} %iota_compare_fusion.4, f32[1,256,80,64]{1,3,2,0:T(8,128)} %get-tuple-element.928, ...), kind=kOutput, calls=%fused_computation.34.clone.1 | convolution fusion | flops 4085407744 | bytes 11403264 | tf_op jit(solution)/shard_map/transpose(jvp())/while/body/eval_jaxpr/checkpoint/while/body/eval_jaxpr/checkpoint/btsh,bshp->bthp/dot_general | solution.py:21
  1265.1 8.4 fusion.176
  1277.1 21.9 %multiply_reduce_fusion.6 = (f32[256,80]{0,1:T(8,128)S(1)}, f32[80]{0:T(128)S(1)}, f32[1,256,80,64]{1,3,2,0:T(8,128)S(1)}) fusion(f32[1,256,80,64]{1,3,2,0:T(8,128)} %get-tuple-element.928, f32[1,256,80,64]{1,3,2,0:T(8,128)} %get-tuple-element.929, f32[256,256]{1,0:T(8,128)S(1)} %fusion.175, f32[256,80]{0,1:T(8,128)S(1)} %copy.259, ...), kind=kOutput, calls=%fused_computation.58.clone.1 | convolution fusion | flops 4055347200 | bytes 21545280 | tf_op jit(solution)/shard_map/transpose(jvp())/while/body/eval_jaxpr/checkpoint/while/body/eval_jaxpr/checkpoint/btsh,bshp->bthp/dot_general | solution.py:21
  1301.7 8.0 fusion.184
  1309.8 7.0 bitcast_add_fusion.14
  1316.8 4.5 fusion.179
  1329.1 9.1 constant_dynamic-slice_fusion.6
  1338.1 7.6 copy_bitcast_fusion.6
  1346.7 3.5 dynamic-slice_bitcast_fusion.8
  1352.6 11.4 fusion.185
  1364.6 32.5 %fusion.178 = (f32[256,80]{0,1:T(8,128)S(1)}, f32[256,80]{0,1:T(8,128)S(1)}, f32[256,256]{1,0:T(8,128)S(1)}) fusion(f32[256,80]{0,1:T(8,128)S(1)} %copy.259, f32[256,256]{1,0:T(8,128)S(1)} %fusion.175, pred[256,256]{1,0:T(8,128)(4,1)S(1)} %iota_compare_fusion.4, f32[1,256,80,64]{1,3,2,0:T(8,128)} %get-tuple-element.928, ...), kind=kOutput, calls=%fused_computation.34.clone.1 | convolution fusion | flops 4085407744 | bytes 11403264 | tf_op jit(solution)/shard_map/transpose(jvp())/while/body/eval_jaxpr/checkpoint/while/body/eval_jaxpr/checkpoint/btsh,bshp->bthp/dot_general | solution.py:21
  1397.6 8.4 fusion.176
  1409.6 22.1 %multiply_reduce_fusion.6 = (f32[256,80]{0,1:T(8,128)S(1)}, f32[80]{0:T(128)S(1)}, f32[1,256,80,64]{1,3,2,0:T(8,128)S(1)}) fusion(f32[1,256,80,64]{1,3,2,0:T(8,128)} %get-tuple-element.928, f32[1,256,80,64]{1,3,2,0:T(8,128)} %get-tuple-element.929, f32[256,256]{1,0:T(8,128)S(1)} %fusion.175, f32[256,80]{0,1:T(8,128)S(1)} %copy.259, ...), kind=kOutput, calls=%fused_computation.58.clone.1 | convolution fusion | flops 4055347200 | bytes 21545280 | tf_op jit(solution)/shard_map/transpose(jvp())/while/body/eval_jaxpr/checkpoint/while/body/eval_jaxpr/checkpoint/btsh,bshp->bthp/dot_general | solution.py:21
  1434.4 8.0 fusion.184
  1442.4 7.1 bitcast_add_fusion.14
  1449.5 4.5 fusion.179
  1463.4 7.3 copy.213
  1472.4 38.5 %all-reduce.2 = (f32[80]{0:T(128)}, f32[80]{0:T(128)}) all-reduce(f32[80]{0:T(128)S(1)} %negate_multiply_fusion, f32[80]{0:T(128)S(1)} %get-tuple-element.475), channel_id=1, replica_groups=mesh['cp'=32] {'cp'}, use_global_device_ids=true, to_apply=%region_23.24 | all-reduce | flops 160 | bytes 1280 | tf_op jit(solution)/shard_map/psum | solution.py:90
  (282 shorter events, 89.1 us)
Async XLA Ops:
  7.2 454.3 %all-gather.7.cloned.1.call-start = ((), (), s32[]{:S(2)}) async-start(), calls=%async_computation.1 | async-start | bytes 86507520 | tf_op jit(solution)/shard_map/all_gather | solution.py:81
  11.4 11.7 copy-start.5
  11.5 11.8 copy-start.7
  22.9 875.9 %all-gather.5.cloned.1.call-start = ((), (), s32[]{:S(2)}) async-start(), calls=%async_computation | async-start | bytes 86507520 | tf_op jit(solution)/shard_map/all_gather | solution.py:80
  57.7 68.0 %copy-start.8 = (bf16[1,768,128]{2,1,0:T(8,128)(2,1)S(1)}, bf16[1,768,128]{2,1,0:T(8,128)(2,1)}, u32[]{:S(2)}) copy-start(bf16[1,768,128]{2,1,0:T(8,128)(2,1)} %param.17) | copy-start | bytes 589828
  898.8 103.6 %copy-start.3 = (f32[1,80,64,128]{3,2,1,0:T(8,128)S(1)}, f32[1,80,64,128]{3,2,1,0:T(8,128)}, u32[]{:S(2)}) copy-start(f32[1,80,64,128]{3,2,1,0:T(8,128)} %param.19) | copy-start | bytes 7864324
  1002.4 1.7 copy-start.1
  1002.4 2.5 copy-start.2
  1002.4 3.3 copy-start.4
  1058.1 5.6 copy-start.11
  1063.7 399.6 %copy-start.12 = (f32[80]{0:T(128)S(1)}, f32[80]{0:T(128)}, u32[]{:S(2)}) copy-start(f32[80]{0:T(128)} %param.15) | copy-start | bytes 964
  1087.4 45.1 %slice-start.2 = ((s8[5242880]{0:T(1024)(128)(4,1)}), s8[1048576]{0:T(1024)(128)(4,1)S(1)}, s32[]{:S(2)}) async-start(s8[5242880]{0:T(1024)(128)(4,1)} %bitcast.512), calls=%async_computation.4 | async-start | bytes 2097152 | tf_op jit(solution)/shard_map/transpose(jvp())/while/body/eval_jaxpr/checkpoint/while
  1099.3 32.8 %copy-start.9 = (bf16[3,1,256,128]{3,2,1,0:T(8,128)(2,1)S(1)}, bf16[3,1,256,128]{3,2,1,0:T(8,128)(2,1)}, u32[]{:S(2)}) copy-start(bf16[3,1,256,128]{3,2,1,0:T(8,128)(2,1)} %get-tuple-element.1007) | copy-start | bytes 589828 | tf_op jit(solution)/shard_map/transpose(jvp())/while/body/eval_jaxpr/checkpoint/while
  1099.4 33.2 %slice-start.3 = ((s8[5242880]{0:T(1024)(128)(4,1)}), s8[4194304]{0:T(1024)(128)(4,1)S(1)}, s32[]{:S(2)}) async-start(s8[5242880]{0:T(1024)(128)(4,1)} %bitcast.512), calls=%async_computation.5 | async-start | bytes 8388608 | tf_op jit(solution)/shard_map/transpose(jvp())/while/body/eval_jaxpr/checkpoint/while
  1132.6 8.4 copy-start.10
  1141.1 25.4 %slice-start = ((s8[5242880]{0:T(1024)(128)(4,1)}), s8[1048576]{0:T(1024)(128)(4,1)S(1)}, s32[]{:S(2)}) async-start(s8[5242880]{0:T(1024)(128)(4,1)} %bitcast.510), calls=%async_computation.2 | async-start | bytes 2097152 | tf_op jit(solution)/shard_map/transpose(jvp())/while/body/eval_jaxpr/checkpoint/while
  1144.6 21.9 %slice-start.1 = ((s8[5242880]{0:T(1024)(128)(4,1)}), s8[4194304]{0:T(1024)(128)(4,1)S(1)}, s32[]{:S(2)}) async-start(s8[5242880]{0:T(1024)(128)(4,1)} %bitcast.510), calls=%async_computation.3 | async-start | bytes 8388608 | tf_op jit(solution)/shard_map/transpose(jvp())/while/body/eval_jaxpr/checkpoint/while
  1177.3 7.1 copy-start
  1220.0 45.1 %slice-start.2 = ((s8[5242880]{0:T(1024)(128)(4,1)}), s8[1048576]{0:T(1024)(128)(4,1)S(1)}, s32[]{:S(2)}) async-start(s8[5242880]{0:T(1024)(128)(4,1)} %bitcast.512), calls=%async_computation.4 | async-start | bytes 2097152 | tf_op jit(solution)/shard_map/transpose(jvp())/while/body/eval_jaxpr/checkpoint/while
  1231.9 32.8 %copy-start.9 = (bf16[3,1,256,128]{3,2,1,0:T(8,128)(2,1)S(1)}, bf16[3,1,256,128]{3,2,1,0:T(8,128)(2,1)}, u32[]{:S(2)}) copy-start(bf16[3,1,256,128]{3,2,1,0:T(8,128)(2,1)} %get-tuple-element.1007) | copy-start | bytes 589828 | tf_op jit(solution)/shard_map/transpose(jvp())/while/body/eval_jaxpr/checkpoint/while
  1231.9 33.2 %slice-start.3 = ((s8[5242880]{0:T(1024)(128)(4,1)}), s8[4194304]{0:T(1024)(128)(4,1)S(1)}, s32[]{:S(2)}) async-start(s8[5242880]{0:T(1024)(128)(4,1)} %bitcast.512), calls=%async_computation.5 | async-start | bytes 8388608 | tf_op jit(solution)/shard_map/transpose(jvp())/while/body/eval_jaxpr/checkpoint/while
  1265.1 8.4 copy-start.10
  1273.6 25.4 %slice-start = ((s8[5242880]{0:T(1024)(128)(4,1)}), s8[1048576]{0:T(1024)(128)(4,1)S(1)}, s32[]{:S(2)}) async-start(s8[5242880]{0:T(1024)(128)(4,1)} %bitcast.510), calls=%async_computation.2 | async-start | bytes 2097152 | tf_op jit(solution)/shard_map/transpose(jvp())/while/body/eval_jaxpr/checkpoint/while
  1277.1 22.0 %slice-start.1 = ((s8[5242880]{0:T(1024)(128)(4,1)}), s8[4194304]{0:T(1024)(128)(4,1)S(1)}, s32[]{:S(2)}) async-start(s8[5242880]{0:T(1024)(128)(4,1)} %bitcast.510), calls=%async_computation.3 | async-start | bytes 8388608 | tf_op jit(solution)/shard_map/transpose(jvp())/while/body/eval_jaxpr/checkpoint/while
  1309.7 7.1 copy-start
  1352.6 44.9 %slice-start.2 = ((s8[5242880]{0:T(1024)(128)(4,1)}), s8[1048576]{0:T(1024)(128)(4,1)S(1)}, s32[]{:S(2)}) async-start(s8[5242880]{0:T(1024)(128)(4,1)} %bitcast.512), calls=%async_computation.4 | async-start | bytes 2097152 | tf_op jit(solution)/shard_map/transpose(jvp())/while/body/eval_jaxpr/checkpoint/while
  1364.5 32.6 %copy-start.9 = (bf16[3,1,256,128]{3,2,1,0:T(8,128)(2,1)S(1)}, bf16[3,1,256,128]{3,2,1,0:T(8,128)(2,1)}, u32[]{:S(2)}) copy-start(bf16[3,1,256,128]{3,2,1,0:T(8,128)(2,1)} %get-tuple-element.1007) | copy-start | bytes 589828 | tf_op jit(solution)/shard_map/transpose(jvp())/while/body/eval_jaxpr/checkpoint/while
  1364.5 33.0 %slice-start.3 = ((s8[5242880]{0:T(1024)(128)(4,1)}), s8[4194304]{0:T(1024)(128)(4,1)S(1)}, s32[]{:S(2)}) async-start(s8[5242880]{0:T(1024)(128)(4,1)} %bitcast.512), calls=%async_computation.5 | async-start | bytes 8388608 | tf_op jit(solution)/shard_map/transpose(jvp())/while/body/eval_jaxpr/checkpoint/while
  1397.6 8.4 copy-start.10
  1406.1 25.6 %slice-start = ((s8[5242880]{0:T(1024)(128)(4,1)}), s8[1048576]{0:T(1024)(128)(4,1)S(1)}, s32[]{:S(2)}) async-start(s8[5242880]{0:T(1024)(128)(4,1)} %bitcast.510), calls=%async_computation.2 | async-start | bytes 2097152 | tf_op jit(solution)/shard_map/transpose(jvp())/while/body/eval_jaxpr/checkpoint/while
  1409.6 22.1 %slice-start.1 = ((s8[5242880]{0:T(1024)(128)(4,1)}), s8[4194304]{0:T(1024)(128)(4,1)S(1)}, s32[]{:S(2)}) async-start(s8[5242880]{0:T(1024)(128)(4,1)} %bitcast.510), calls=%async_computation.3 | async-start | bytes 8388608 | tf_op jit(solution)/shard_map/transpose(jvp())/while/body/eval_jaxpr/checkpoint/while
  1442.4 7.1 copy-start
  1463.4 7.3 copy-start.6
Sparse Core Ops, SparseCore 0:
  23.1 438.3 all-gather.6
  464.3 434.4 all-gather.4
where the time goes:
time: 1530 us; the launch traced here: 1520 us
  matrix products  642 us (42%)
  waiting for transfers between devices  561 us (37%)
  local copies, waits for them, and re-layouts  170 us (11%)
  blocking collectives  82 us (5%)
  other arithmetic  44 us (3%)
    all_gather x1, waiting for transfers between devices, device_step(): grad_all = lax.all_gather(grad_part, AXIS)  335 us
    all_gather x1, waiting for transfers between devices, device_step(): state_all = lax.all_gather(state_part, AXIS)  226 us
    dot_general x6, matrix products, chunk_step(): jnp.einsum('btsh,bshp->bthp', mix_mat, u_blk, precision=HIGH_PREC, prefer...  164 us
    dot_general x1, matrix products, link_states(): jnp.einsum('jbh,jbhpn->bhpn', w_right, grad_all, precision=HIGH_PREC, pre...  106 us
    dot_general x1, matrix products, link_states(): jnp.einsum('jbh,jbhpn->bhpn', jnp.exp(log_before), grad_all, precision=HI...  106 us
    dot_general x1, matrix products, link_states(): jnp.einsum('jbh,jbhpn->bhpn', w_left, state_all, precision=HIGH_PREC, pre...  104 us
    dot_general x9, matrix products, chunk_step(): jnp.einsum('bhpn,btn->bthp', carry_state, c_blk, precision=HIGH_PREC, pre...  68.7 us
    dot_general x9, matrix products, chunk_step(): jnp.einsum('bsh,bshp,bsn->bhpn', tail_decay, u_blk, b_blk, precision=HIGH...  67.9 us
  transfers between devices with their start and end apart: 2, of which 2 were waited for; matrix products, arithmetic and copies ran while one was open for 18% of the time, Pallas kernels for 0%

commit v1 on v0

v1 whole, which is shorter than its diff:
```python
import functools
import jax
import jax.numpy as jnp
from jax import lax
from jax.experimental import pallas as pl
from jax.experimental.pallas import tpu as pltpu
from jax.sharding import PartitionSpec as P

AXIS = 'cp'
H, PD, N = 80, 64, 128
L = 128
HG = 8
LOG2E = 1.4426950408889634
NEG = -1e30
F32, BF16 = jnp.float32, jnp.bfloat16
HIGHEST = lax.Precision.HIGHEST
NT = (((1,), (1,)), ((), ()))
TN = (((0,), (0,)), ((), ()))
NN = (((1,), (0,)), ((), ()))


def dot(a, b, dims=NN, precision=None):
    return lax.dot_general(a, b, dims, precision=precision, preferred_element_type=F32)


def split(v):
    hi = v.astype(BF16)
    return hi, (v - hi.astype(F32)).astype(BF16)


MESH = pl.DeviceIdType.MESH


def greet_all(nd, me):
    barrier = pltpu.get_barrier_semaphore()
    for o in range(1, nd):
        pl.semaphore_signal(barrier, inc=1, device_id=(lax.rem(me + o, nd),), device_id_type=MESH)
    pl.semaphore_wait(barrier, nd - 1)


def tile_copy(nd, me, o, got, send, recv):
    return pltpu.make_async_remote_copy(src_ref=got.at[me], dst_ref=got.at[me], send_sem=send.at[o], recv_sem=recv.at[o],
                                        device_id=(lax.rem(me + o, nd),), device_id_type=MESH)


def send_all(nd, me, got, send, recv):
    for o in range(1, nd):
        tile_copy(nd, me, o, got, send, recv).start()


def wait_all(nd, me, got, send, recv):
    for o in range(1, nd):
        src = lax.rem(me + nd - o, nd)
        pltpu.make_async_remote_copy(src_ref=got.at[src], dst_ref=got.at[src], send_sem=send.at[o], recv_sem=recv.at[o],
                                     device_id=(src,), device_id_type=MESH).wait_recv()
        tile_copy(nd, me, o, got, send, recv).wait_send()


def summary_kernel(nd, x_ref, dy_ref, dt_ref, par_ref, b_ref, c_ref, s_ref, g_ref, cs_ref, tot_ref, all_ref,
                   tu_hi, tu_lo, sd_hi, sd_lo, cs_all, off_all, got, send, recv):
    nb = x_ref.shape[2] // L
    g = pl.program_id(0)
    me = lax.axis_index(AXIS)

    @pl.when(g == 0)
    def _():
        tri = (lax.broadcasted_iota(jnp.int32, (L, L), 0) <= lax.broadcasted_iota(jnp.int32, (L, L), 1)).astype(F32)
        off = jnp.zeros((H, L), F32)
        for b in range(nb):
            sl = slice(b * L, (b + 1) * L)
            a = dt_ref[:, sl] * (par_ref[:, 0:1] * LOG2E)
            cs = dot(a, tri, precision=HIGHEST)
            cs_all[:, sl] = cs
            off_all[:, sl] = off
            off = off + jnp.broadcast_to(cs[:, L - 1:L], (H, L))
        off_all[:, nb * L:] = off
        cs_ref[...] = cs_all[...]
        tot_ref[...] = off
        got[me] = jnp.transpose(jnp.concatenate([off, jnp.zeros((L - H, L), F32)], axis=0))[:8]
        greet_all(nd, me)
        send_all(nd, me, got, send, recv)

    rows = pl.ds(pl.multiple_of(g * HG, HG), HG)
    for b in range(nb):
        sl = slice(b * L, (b + 1) * L)
        run = cs_all[rows, sl] + off_all[rows, sl]
        ec = jnp.exp2(run)
        tl = jnp.exp2(off_all[rows, nb * L:] - run) * dt_ref[rows, sl]
        for j in range(HG):
            pr = slice(j * PD, (j + 1) * PD)
            tu_hi[pr, sl], tu_lo[pr, sl] = split(x_ref[j, :, sl].astype(F32) * tl[j:j + 1])
            sd_hi[pr, sl], sd_lo[pr, sl] = split(dy_ref[j, :, sl].astype(F32) * ec[j:j + 1])
    s_ref[...] = dot(tu_hi[...], b_ref[...]) + dot(tu_lo[...], b_ref[...])
    g_ref[...] = dot(sd_hi[...], c_ref[...]) + dot(sd_lo[...], c_ref[...])

    @pl.when(g == pl.num_programs(0) - 1)
    def _():
        wait_all(nd, me, got, send, recv)
        all_ref[...] = got[...]


def summaries(nd, x, dy, dt, par, b, c):
    t = x.shape[2]
    full = lambda shape: pl.BlockSpec(shape, lambda g: (0,) * len(shape))
    heads = pl.BlockSpec((HG, PD, t), lambda g: (g, 0, 0))
    state = pl.BlockSpec((HG * PD, N), lambda g: (g, 0))
    half = pltpu.VMEM((HG * PD, t), BF16)
    return pl.pallas_call(
        functools.partial(summary_kernel, nd),
        grid=(H // HG,),
        in_specs=[heads, heads, full((H, t)), full((H, L)), full((t, N)), full((t, N))],
        out_specs=[state, state, full((H, t)), full((H, L)), full((nd, 8, L))],
        out_shape=[jax.ShapeDtypeStruct((H * PD, N), F32), jax.ShapeDtypeStruct((H * PD, N), F32),
                   jax.ShapeDtypeStruct((H, t), F32), jax.ShapeDtypeStruct((H, L), F32), jax.ShapeDtypeStruct((nd, 8, L), F32)],
        scratch_shapes=[half, half, half, half, pltpu.VMEM((H, t), F32), pltpu.VMEM((H, t + L), F32), pltpu.VMEM((nd, 8, L), F32),
                        pltpu.SemaphoreType.DMA((nd,)), pltpu.SemaphoreType.DMA((nd,))],
        compiler_params=pltpu.CompilerParams(dimension_semantics=("arbitrary",), collective_id=1, has_side_effects=True),
        cost_estimate=pl.CostEstimate(flops=4 * H * PD * N * t * 2, bytes_accessed=4 * H * PD * t, transcendentals=0),
        name="range_summaries",
    )(x, dy, dt, par, b, c)


def tile_sum_kernel(nd, dh_ref, out_ref, got, send, recv):
    me = lax.axis_index(AXIS)
    got[me] = jnp.transpose(jnp.concatenate([dh_ref[...], jnp.zeros((L - H, L), F32)], axis=0))[:8]
    greet_all(nd, me)
    send_all(nd, me, got, send, recv)
    wait_all(nd, me, got, send, recv)
    total = got[0]
    for d in range(1, nd):
        total = total + got[d]
    out_ref[...] = total


def tile_sum(nd, dh):
    vm = pl.BlockSpec(memory_space=pltpu.VMEM)
    return pl.pallas_call(
        functools.partial(tile_sum_kernel, nd),
        in_specs=[vm], out_specs=vm, out_shape=jax.ShapeDtypeStruct((8, L), F32),
        scratch_shapes=[pltpu.VMEM((nd, 8, L), F32), pltpu.SemaphoreType.DMA((nd,)), pltpu.SemaphoreType.DMA((nd,))],
        compiler_params=pltpu.CompilerParams(collective_id=2, has_side_effects=True),
        name="tile_sum",
    )(dh)


CH = 2
KC = H // CH
HOP = 3


def chain_kernel(nd, tot_ref, s_ref, g_ref, s0_ref, g0_ref, so_ref, go_ref, s_out, g_out, s_send, s_recv, g_send, g_recv):
    me = lax.axis_index(AXIS)
    right, left = lax.rem(me + 1, nd), lax.rem(me + nd - 1, nd)
    barrier = pltpu.get_barrier_semaphore()
    for other in (left, right):
        pl.semaphore_signal(barrier, inc=1, device_id=(other,), device_id_type=pl.DeviceIdType.MESH)
    pl.semaphore_wait(barrier, 2)
    rows_of = lambda k: pl.ds(pl.multiple_of(k * CH * PD, CH * PD), CH * PD)

    def copy(out, into, send, recv, k, to):
        return pltpu.make_async_remote_copy(src_ref=out.at[rows_of(k)], dst_ref=into.at[rows_of(k)], send_sem=send.at[k], recv_sem=recv.at[k],
                                            device_id=(to,), device_id_type=pl.DeviceIdType.MESH)

    def pass_on(k, edge, last, to, first_ref, own_ref, into, out, send, recv):
        rows = rows_of(k)

        @pl.when(edge)
        def _():
            into[rows] = first_ref[rows]

        @pl.when(jnp.logical_not(edge))
        def _():
            copy(out, into, send, recv, k, to).wait_recv()

        @pl.when(jnp.logical_not(last))
        def _():
            for i in range(CH):
                r = pl.ds(pl.multiple_of(k * CH * PD + i * PD, PD), PD)
                decay = jnp.exp2(tot_ref[pl.ds(k * CH + i, 1), :])
                out[r] = decay * into[r] + own_ref[r]
            copy(out, into, send, recv, k, to).start()

    def step(n, _):
        ks, kg = n - HOP * me, n - HOP * (nd - 1 - me)

        @pl.when((ks >= 0) & (ks < KC))
        def _():
            pass_on(ks, me == 0, me == nd - 1, right, s0_ref, s_ref, so_ref, s_out, s_send, s_recv)

        @pl.when((kg >= 0) & (kg < KC))
        def _():
            pass_on(kg, me == nd - 1, me == 0, left, g0_ref, g_ref, go_ref, g_out, g_send, g_recv)
        return 0

    lax.fori_loop(0, HOP * (nd - 1) + KC, step, 0)

    def drain(k, _):
        @pl.when(me < nd - 1)
        def _():
            copy(s_out, so_ref, s_send, s_recv, k, right).wait_send()

        @pl.when(me > 0)
        def _():
            copy(g_out, go_ref, g_send, g_recv, k, left).wait_send()
        return 0

    lax.fori_loop(0, KC, drain, 0)


def chain(nd, tot, s_loc, g_loc, s0, g0):
    vm = pl.BlockSpec(memory_space=pltpu.VMEM)
    state = jax.ShapeDtypeStruct((H * PD, N), F32)
    return pl.pallas_call(
        functools.partial(chain_kernel, nd),
        in_specs=[vm] * 5,
        out_specs=[vm] * 2,
        out_shape=[state, state],
        scratch_shapes=[pltpu.VMEM((H * PD, N), F32), pltpu.VMEM((H * PD, N), F32)] + [pltpu.SemaphoreType.DMA((KC,))] * 4,
        compiler_params=pltpu.CompilerParams(collective_id=0, has_side_effects=True),
        cost_estimate=pl.CostEstimate(flops=10 ** 10, bytes_accessed=10 ** 7, transcendentals=0),
        name="state_chain",
    )(tot, s_loc, g_loc, s0, g0)


def local_kernel(x_ref, dy_ref, dt_ref, cs_ref, s0_ref, g1_ref, b_ref, c_ref, par_ref, dta_ref, para_ref,
                 dx_ref, ddt_ref, db_ref, dc_ref, dh_ref,
                 sf, gc, tu, sd, gh, us, gram, dg_acc, db_acc, dc_acc, ec_s, td_s, tl_s, ddir_s, xd_s, dcs_s, kd_s,
                 bb_ref, cc_ref, b2t_ref, ct_ref):
    nb = x_ref.shape[2] // L
    g = pl.program_id(0)
    below = lax.broadcasted_iota(jnp.int32, (L, L), 0) >= lax.broadcasted_iota(jnp.int32, (L, L), 1)
    lane = lax.broadcasted_iota(jnp.int32, (L, L), 1)

    @pl.when(g == 0)
    def _():
        for b in range(nb):
            bb, cc = b_ref[b * L:(b + 1) * L, :], c_ref[b * L:(b + 1) * L, :]
            gram[b] = dot(cc, bb, NT)
            bb_ref[b] = jnp.concatenate([bb, bb], axis=0)
            cc_ref[b] = jnp.concatenate([cc, cc], axis=0)
            bt = jnp.transpose(bb.astype(F32)).astype(BF16)
            b2t_ref[b] = jnp.concatenate([bt, bt], axis=0)
            ct_ref[b] = jnp.transpose(cc.astype(F32))
        dg_acc[...] = jnp.zeros_like(dg_acc)
        db_acc[...] = jnp.zeros_like(db_acc)
        dc_acc[...] = jnp.zeros_like(dc_acc)

    heads = pl.ds(pl.multiple_of(g * HG, HG), HG)
    for b in range(nb):
        sl = slice(b * L, (b + 1) * L)
        cs = cs_ref[:, sl]
        tail = jnp.exp2(cs[:, L - 1:L] - cs)
        ec_s[b] = jnp.exp2(cs)
        tl_s[b] = tail
        td_s[b] = tail * dt_ref[:, sl]

    sf[0] = s0_ref[...]

    def forward(b, _):
        toks = pl.ds(pl.multiple_of(b * L, L), L)
        etot = ec_s[b][:, L - 1:L]
        td = td_s[b]
        for j in range(HG):
            hi, lo = split(x_ref[j, :, toks].astype(F32) * td[j:j + 1])
            tu[b, j * PD:(j + 1) * PD, :L] = hi
            tu[b, j * PD:(j + 1) * PD, L:] = lo
        new = dot(tu[b], bb_ref[b])
        for j in range(HG):
            pr = slice(j * PD, (j + 1) * PD)
            sf[b + 1, pr] = etot[j:j + 1] * sf[b, pr] + new[pr]
        return 0

    lax.fori_loop(0, nb, forward, 0)
    gc[...] = g1_ref[...]

    def backward(i, _):
        b = nb - 1 - i
        toks = pl.ds(pl.multiple_of(b * L, L), L)
        ec, tl, cs, dtb = ec_s[b], tl_s[b], cs_ref[:, toks], dt_ref[:, toks]
        etot = ec[:, L - 1:L]
        cst = jnp.transpose(cs)
        kd = []
        for j in range(HG):
            pr = slice(j * PD, (j + 1) * PD)
            gj = gc[pr]
            kd.append(jnp.sum(gj * sf[b + 1, pr], axis=0, keepdims=True))
            hi, lo = split(gj)
            gh[pr, :L] = hi
            gh[pr, L:] = lo
            hi, lo = split(dy_ref[j, :, toks].astype(F32) * ec[j:j + 1])
            sd[pr, :L] = hi
            sd[pr, L:] = lo
        kd_s[b, heads] = jnp.concatenate(kd, axis=0)
        us[...] = dot(gh[...], b2t_ref[b])
        db_acc[b] += (dot(gh[:, :L], tu[b, :, :L], TN) + dot(gh[:, L:], tu[b, :, :L], TN)) + dot(gh[:, :L], tu[b, :, L:], TN)
        gram_b = gram[b]
        ct = ct_ref[b]
        dg = jnp.zeros((L, L), F32)
        dc = jnp.zeros((N, L), F32)
        rs_cols = jnp.zeros((L, L), F32)
        ddir, xd, inter = [], [], []
        for j in range(HG):
            pr = slice(j * PD, (j + 1) * PD)
            xj, dyj = x_ref[j, :, toks], dy_ref[j, :, toks]
            e = jnp.exp2(jnp.where(below, jnp.broadcast_to(cst[:, j:j + 1], (L, L)) - cs[j:j + 1], NEG))
            m = gram_b * e
            mhi, mlo = split(m)
            du = dot(jnp.concatenate([dyj, dyj], axis=1), jnp.concatenate([mhi, mlo], axis=0)) + us[pr] * tl[j:j + 1]
            dp = dot(dyj, xj, TN)
            w = dp * (e * dtb[j:j + 1])
            dg = dg + w
            rs = jnp.sum(w * gram_b, axis=1, keepdims=True)
            rs_cols = jnp.where(lane == j, jnp.broadcast_to(rs, (L, L)), rs_cols)
            xf, dyf = xj.astype(F32), dyj.astype(F32)
            ddir.append(jnp.sum(du * xf, axis=0, keepdims=True))
            xd.append(jnp.sum(dyf * xf, axis=0, keepdims=True))
            dx_ref[j, :, toks] = (du * dtb[j:j + 1] + dyf * par_ref[j:j + 1, 1:2]).astype(BF16)
            shi, slo = split(sf[b, pr])
            st = jnp.transpose(jnp.concatenate([shi, slo, shi, slo], axis=0))
            dhi, dlo = sd[pr, :L], sd[pr, L:]
            z = dot(st, jnp.concatenate([dhi, dhi, dlo, dlo], axis=0))
            dc = dc + z
            inter.append(jnp.sum(z * ct, axis=0, keepdims=True))
        dg_acc[b] += dg
        dc_acc[b] += dc
        ddir = jnp.concatenate(ddir, axis=0)
        ddir_s[b, heads] = ddir
        xd_s[b, heads] = jnp.concatenate(xd, axis=0)
        dcs_s[b, heads] = jnp.transpose(rs_cols)[:HG] + jnp.concatenate(inter, axis=0) - ddir * dtb
        grow = dot(sd[...], cc_ref[b])
        for j in range(HG):
            pr = slice(j * PD, (j + 1) * PD)
            gc[pr] = etot[j:j + 1] * gc[pr] + grow[pr]
        return 0

    lax.fori_loop(0, nb, backward, 0)

    @pl.when(g == pl.num_programs(0) - 1)
    def _():
        after = below.astype(F32)
        da_sum = jnp.zeros((H, 1), F32)
        dd_sum = jnp.zeros((H, 1), F32)
        for b in range(nb):
            sl = slice(b * L, (b + 1) * L)
            da = dot(dcs_s[b], after, precision=HIGHEST) + jnp.sum(kd_s[b], axis=1, keepdims=True)
            dta = da * para_ref[:, 0:1]
            ddt_ref[:, sl] = ddir_s[b] + dta
            da_sum += jnp.sum(dta * dta_ref[:, sl], axis=1, keepdims=True)
            dd_sum += jnp.sum(xd_s[b], axis=1, keepdims=True)
            ghi, glo = split(dg_acc[b])
            dbt = jnp.transpose(db_acc[b]) + (dot(ghi, cc_ref[b, :L, :], TN) + dot(glo, cc_ref[b, :L, :], TN))
            dct = jnp.transpose(dc_acc[b]) + (dot(ghi, bb_ref[b, :L, :]) + dot(glo, bb_ref[b, :L, :]))
            db_ref[sl, :] = dbt.astype(BF16)
            dc_ref[sl, :] = dct.astype(BF16)
        lane_h = lax.broadcasted_iota(jnp.int32, (H, L), 1)
        dh_ref[...] = jnp.where(lane_h == 0, da_sum, jnp.where(lane_h == 1, dd_sum, 0.0))


def local_backward(x, dy, dt, cs, s_start, ds_end, b, c, par):
    t = x.shape[2]
    nb = t // L
    full = lambda shape: pl.BlockSpec(shape, lambda g: (0,) * len(shape))
    heads = pl.BlockSpec((HG, PD, t), lambda g: (g, 0, 0))
    rows = pl.BlockSpec((HG, t), lambda g: (g, 0))
    state = pl.BlockSpec((HG * PD, N), lambda g: (g, 0))
    one = pl.BlockSpec((HG, L), lambda g: (g, 0))
    vm = lambda shape, dtype=F32: pltpu.VMEM(shape, dtype)
    return pl.pallas_call(
        local_kernel,
        grid=(H // HG,),
        in_specs=[heads, heads, rows, rows, state, state, full((t, N)), full((t, N)), one, full((H, t)), full((H, L))],
        out_specs=[heads, full((H, t)), full((t, N)), full((t, N)), full((H, L))],
        out_shape=[jax.ShapeDtypeStruct((H, PD, t), BF16), jax.ShapeDtypeStruct((H, t), F32), jax.ShapeDtypeStruct((t, N), BF16),
                   jax.ShapeDtypeStruct((t, N), BF16), jax.ShapeDtypeStruct((H, L), F32)],
        scratch_shapes=[vm((nb + 1, HG * PD, N)), vm((HG * PD, N)), vm((nb, HG * PD, 2 * L), BF16), vm((HG * PD, 2 * L), BF16),
                        vm((HG * PD, 2 * N), BF16), vm((HG * PD, L)), vm((nb, L, L)), vm((nb, L, L)), vm((nb, N, L)), vm((nb, N, L)),
                        vm((nb, HG, L)), vm((nb, HG, L)), vm((nb, HG, L)), vm((nb, H, L)), vm((nb, H, L)), vm((nb, H, L)), vm((nb, H, N)),
                        vm((nb, 2 * L, N), BF16), vm((nb, 2 * L, N), BF16), vm((nb, 2 * N, L), BF16), vm((nb, N, L))],
        compiler_params=pltpu.CompilerParams(dimension_semantics=("arbitrary",)),
        cost_estimate=pl.CostEstimate(flops=5 * 10 ** 10, bytes_accessed=6 * H * PD * t, transcendentals=H * t * L),
        name="local_backward",
    )(x, dy, dt, cs, s_start, ds_end, b, c, par, dt, par)


def solution(mesh):
    nd = mesh.shape[AXIS]
    tok4 = P(None, AXIS, None, None)
    tok3 = P(None, AXIS, None)

    def device_step(x_loc, dt_loc, a_log, b_loc, c_loc, d_skip, s_init, dy_loc, ds_last):
        x, dy = jnp.transpose(x_loc[0], (1, 2, 0)), jnp.transpose(dy_loc[0], (1, 2, 0))
        dt = jnp.transpose(dt_loc[0])
        b, c = b_loc[0], c_loc[0]
        col = jnp.arange(L)[None, :]
        par = jnp.where(col == 0, -jnp.exp(a_log)[:, None], jnp.where(col == 1, d_skip[:, None], 0.0))
        s_loc, g_loc, cs, tot, tot_all = summaries(nd, x, dy, dt, par, b, c)
        s0, g0 = s_init.reshape(H * PD, N), ds_last.reshape(H * PD, N)

        tot_all = tot_all[:, 0, :H]
        before = jnp.sum(jnp.where(jnp.arange(nd)[:, None] < lax.axis_index(AXIS), tot_all, 0.0), axis=0)
        part = jnp.exp2(before)[:, None, None] * g_loc.reshape(H, PD, N)
        ds_first = jnp.exp2(jnp.sum(tot_all, axis=0))[:, None, None] * ds_last[0] + lax.psum(part, AXIS)

        s_start, ds_end = chain(nd, tot, s_loc, g_loc, s0, g0)
        dx, ddt, db, dc, dh = local_backward(x, dy, dt, cs, s_start, ds_end, b, c, par)
        dh = tile_sum(nd, dh)
        return (jnp.transpose(dx, (2, 0, 1))[None], jnp.transpose(ddt)[None], db[None], dc[None], ds_first[None], dh[0, :H], dh[1, :H])

    return jax.shard_map(device_step, mesh=mesh,
                         in_specs=(tok4, tok3, P(), tok3, tok3, P(), P(), tok4, P()),
                         out_specs=(tok4, tok3, tok3, tok3, P(), P(), P()),
                         check_vma=False)
```

time: 1530 us -> 306 us (0.20)
  matrix products: 642 us -> 0 us
  waiting for transfers between devices: 561 us -> 0.02 us
  Pallas kernels: 0 us -> 280 us
  local copies, waits for them, and re-layouts: 170 us -> 1.28 us
  blocking collectives: 82 us -> 0 us
  other arithmetic: 44 us -> 10.1 us
    dot_general x38 -> x0, matrix products: 642 us -> none  [the longest x6 164 us: chunk_step(): jnp.einsum('btsh,bshp->bthp', mix_mat, u_blk, precision=HIGH_PREC, prefer...]
    all_gather x2 -> x0, waiting for transfers between devices: 561 us -> none  [the longest x1 335 us: device_step(): grad_all = lax.all_gather(grad_part, AXIS)]
    pallas_call x0 -> x4, Pallas kernels: none -> 280 us  [the longest x1 137 us: chain(): pl.pallas_call(functools.partial(chain_kernel, nd), in_specs=[vm] * 5, ou...]
    squeeze x15 -> x1, local copies, waits for them, and re-layouts: 86.1 us -> 1.28 us  [device_step(): dh[1, :H]]
    all_gather x1 -> x0, blocking collectives: 43.5 us -> none  [device_step(): logdec_all = lax.all_gather(log_part, AXIS)]
    psum x1 -> x0, blocking collectives: 38.5 us -> none  [device_step(): grad_alog, grad_skip = lax.psum((grad_alog, grad_skip), AXIS)]
    dynamic_slice x3 -> x0, local copies, waits for them, and re-layouts: 27.2 us -> none  [span_step(): return lax.scan(inner_step, carry_state, span_in)]
  transfers between devices with their start and end apart: 2 -> 1, of which waited for: 2 -> 0; matrix products, arithmetic and copies ran while one was open for 18% -> 0% of each run, Pallas kernels for 0% -> 83%
where the time goes in v1:
time: 306 us
  Pallas kernels  280 us (92%)
  between operations  14.1 us (5%)
  other arithmetic  10.1 us (3%)
    pallas_call x1, Pallas kernels, chain(): pl.pallas_call(functools.partial(chain_kernel, nd), in_specs=[vm] * 5, ou...  137 us
    pallas_call x1, Pallas kernels, local_backward(): pl.pallas_call(local_kernel, grid=(H // HG,), in_specs=[heads, heads, row...  107 us
    pallas_call x1, Pallas kernels, summaries(): pl.pallas_call(functools.partial(summary_kernel, nd), grid=(H // HG,), in...  25.7 us
    pallas_call x1, Pallas kernels, tile_sum(): pl.pallas_call(functools.partial(tile_sum_kernel, nd), in_specs=[vm], out...  10.9 us
  transfers between devices with their start and end apart: 1, of which 0 were waited for; matrix products, arithmetic and copies ran while one was open for 0% of the time, Pallas kernels for 83%

profile of v1, /device:TPU:0, one launch (start us, length us, event | category | flops | bytes accessed | tf_op | source)
XLA Modules:
  0.0 305.7 jit_solution(9975219864820791322)
XLA Ops:
  7.2 0.0 all-reduce.2.cloned.1.call-start
  7.2 0.7 exponential_negate_fusion
  7.9 1.4 select_select_fusion.par_ref.para_ref
  9.3 25.7 %range_summaries.1 = (f32[5120,128]{1,0:T(8,128)}, f32[5120,128]{1,0:T(8,128)}, f32[80,768]{1,0:T(8,128)}, f32[80,128]{1,0:T(8,128)}, f32[32,8,128]{2,1,0:T(8,128)}) custom-call(bf16[80,64,768]{2,1,0:T(8,128)(2,1)} %bitcast.35, bf16[80,64,768]{2,1,0:T(8,128)(2,1)} %bitcast.37, f32[80,768]{1,0:T(8,128)} %bitcast.41, ...), custom_call_target="tpu_custom_call" | custom-call | flops 4026531840 | bytes 15728640 | tf_op jit(solution)/shard_map/range_summaries/pallas_call | solution.py:108
  34.9 1.0 slice_reduce_fusion
  35.9 0.1 select_reduce_fusion
  36.0 3.5 %broadcast_multiply_fusion = f32[80,64,128]{2,1,0:T(8,128)} fusion(f32[80,64,128]{2,1,0:T(8,128)} %bitcast.40, f32[80]{0:T(128)S(1)} %multiply_exponential_fusion), kind=kLoop, calls=%fused_computation.3 | loop fusion | flops 655360 | bytes 5243200 | tf_op jit(solution)/shard_map/mul | solution.py:401
  39.5 0.0 all-reduce.2.cloned.1.call-update
  39.5 136.6 %state_chain.1 = (f32[5120,128]{1,0:T(8,128)}, f32[5120,128]{1,0:T(8,128)}) custom-call(f32[80,128]{1,0:T(8,128)} %get-tuple-element.20.tot_ref, f32[5120,128]{1,0:T(8,128)} %get-tuple-element.21.s_ref, f32[5120,128]{1,0:T(8,128)} %get-tuple-element.22.g_ref, f32[5120,128]{1,0:T(8,128)} %bitcast.49, f32[5120,128]{1,0:T(8,128)} %bitcast.39), custom_call_target="tpu_custom_call" | custom-call | flops 10000000000 | bytes 10000000 | tf_op jit(solution)/shard_map/state_chain/pallas_call | solution.py:213
  176.0 0.0 copy-start
  176.1 107.1 %local_backward.1 = (bf16[80,64,768]{2,1,0:T(8,128)(2,1)}, f32[80,768]{1,0:T(8,128)}, bf16[768,128]{1,0:T(8,128)(2,1)}, bf16[768,128]{1,0:T(8,128)(2,1)}, f32[80,128]{1,0:T(8,128)}) custom-call(bf16[80,64,768]{2,1,0:T(8,128)(2,1)} %bitcast.36, bf16[80,64,768]{2,1,0:T(8,128)(2,1)} %bitcast.38, f32[80,768]{1,0:T(8,128)} %bitcast.42, ...), custom_call_target="tpu_custom_call" | custom-call | flops 49999998976 | bytes 23592960 | tf_op jit(solution)/shard_map/local_backward/pallas_call | solution.py:368
  283.2 10.9 %tile_sum.1 = f32[8,128]{1,0:T(8,128)} custom-call(f32[80,128]{1,0:T(8,128)} %get-tuple-element.30.dh_ref), custom_call_target="tpu_custom_call" | custom-call | tf_op jit(solution)/shard_map/tile_sum/pallas_call | solution.py:137
  294.1 1.3 slice_bitcast_fusion
  295.3 0.0 all-reduce.2.cloned.1.call-done
  295.3 0.0 copy-done
  295.3 3.6 %fusion.1 = f32[1,80,64,128]{3,2,1,0:T(8,128)} fusion(f32[80,64,128]{2,1,0:T(8,128)} %all-reduce.2.cloned.1.call-done, f32[1,80,64,128]{3,2,1,0:T(8,128)S(1)} %copy-done, f32[80]{0:T(128)S(1)} %multiply_exponential_fusion.1), kind=kLoop, calls=%fused_computation.2 | loop fusion | flops 1310720 | bytes 7864640 | tf_op jit(solution)/shard_map/broadcast_in_dim | solution.py:407
  (4 shorter events, 0.0 us)
Async XLA Ops:
  7.2 288.2 %all-reduce.2.cloned.1.call-start = ((), (), s32[]{:S(2)}) async-start(), calls=%async_computation | async-start | bytes 5242880 | tf_op jit(solution)/shard_map/psum | solution.py:402
  176.0 119.3 %copy-start = (f32[1,80,64,128]{3,2,1,0:T(8,128)S(1)}, f32[1,80,64,128]{3,2,1,0:T(8,128)}, u32[]{:S(2)}) copy-start(f32[1,80,64,128]{3,2,1,0:T(8,128)} %param.17) | copy-start | bytes 7864324
Sparse Core Ops, SparseCore 0:
  39.6 147.8 all-reduce.1

commit v2 on v1

v2 whole, which is shorter than its diff:
```python
import functools
import jax
import jax.numpy as jnp
from jax import lax
from jax.experimental import pallas as pl
from jax.experimental.pallas import tpu as pltpu
from jax.sharding import PartitionSpec as P

AXIS = 'cp'
H, PD, N = 80, 64, 128
L = 128
HG = 8
LOG2E = 1.4426950408889634
NEG = -1e30
F32, BF16 = jnp.float32, jnp.bfloat16
HIGHEST = lax.Precision.HIGHEST
NT = (((1,), (1,)), ((), ()))
TN = (((0,), (0,)), ((), ()))
NN = (((1,), (0,)), ((), ()))


def dot(a, b, dims=NN, precision=None):
    return lax.dot_general(a, b, dims, precision=precision, preferred_element_type=F32)


def split(v):
    hi = v.astype(BF16)
    return hi, (v - hi.astype(F32)).astype(BF16)


MESH = pl.DeviceIdType.MESH


def greet_all(nd, me):
    barrier = pltpu.get_barrier_semaphore()
    for o in range(1, nd):
        pl.semaphore_signal(barrier, inc=1, device_id=(lax.rem(me + o, nd),), device_id_type=MESH)
    pl.semaphore_wait(barrier, nd - 1)


def tile_copy(nd, me, o, got, send, recv):
    return pltpu.make_async_remote_copy(src_ref=got.at[me], dst_ref=got.at[me], send_sem=send.at[o], recv_sem=recv.at[o],
                                        device_id=(lax.rem(me + o, nd),), device_id_type=MESH)


def send_all(nd, me, got, send, recv):
    for o in range(1, nd):
        tile_copy(nd, me, o, got, send, recv).start()


def wait_all(nd, me, got, send, recv):
    for o in range(1, nd):
        src = lax.rem(me + nd - o, nd)
        pltpu.make_async_remote_copy(src_ref=got.at[src], dst_ref=got.at[src], send_sem=send.at[o], recv_sem=recv.at[o],
                                     device_id=(src,), device_id_type=MESH).wait_recv()
        tile_copy(nd, me, o, got, send, recv).wait_send()


def summary_kernel(x_ref, dy_ref, dt_ref, par_ref, b_ref, c_ref, s_ref, g_ref, cs_ref, tot_ref,
                   tu_hi, tu_lo, sd_hi, sd_lo, cs_all, off_all):
    nb = x_ref.shape[2] // L
    g = pl.program_id(0)

    @pl.when(g == 0)
    def _():
        tri = (lax.broadcasted_iota(jnp.int32, (L, L), 0) <= lax.broadcasted_iota(jnp.int32, (L, L), 1)).astype(F32)
        off = jnp.zeros((H, L), F32)
        for b in range(nb):
            sl = slice(b * L, (b + 1) * L)
            a = dt_ref[:, sl] * (par_ref[:, 0:1] * LOG2E)
            cs = dot(a, tri, precision=HIGHEST)
            cs_all[:, sl] = cs
            off_all[:, sl] = off
            off = off + jnp.broadcast_to(cs[:, L - 1:L], (H, L))
        off_all[:, nb * L:] = off
        cs_ref[...] = cs_all[...]
        tot_ref[...] = off

    rows = pl.ds(pl.multiple_of(g * HG, HG), HG)
    for b in range(nb):
        sl = slice(b * L, (b + 1) * L)
        run = cs_all[rows, sl] + off_all[rows, sl]
        ec = jnp.exp2(run)
        tl = jnp.exp2(off_all[rows, nb * L:] - run) * dt_ref[rows, sl]
        for j in range(HG):
            pr = slice(j * PD, (j + 1) * PD)
            tu_hi[pr, sl], tu_lo[pr, sl] = split(x_ref[j, :, sl].astype(F32) * tl[j:j + 1])
            sd_hi[pr, sl], sd_lo[pr, sl] = split(dy_ref[j, :, sl].astype(F32) * ec[j:j + 1])
    s_ref[...] = dot(tu_hi[...], b_ref[...]) + dot(tu_lo[...], b_ref[...])
    g_ref[...] = dot(sd_hi[...], c_ref[...]) + dot(sd_lo[...], c_ref[...])


def summaries(x, dy, dt, par, b, c):
    t = x.shape[2]
    full = lambda shape: pl.BlockSpec(shape, lambda g: (0,) * len(shape))
    heads = pl.BlockSpec((HG, PD, t), lambda g: (g, 0, 0))
    state = pl.BlockSpec((HG * PD, N), lambda g: (g, 0))
    half = pltpu.VMEM((HG * PD, t), BF16)
    return pl.pallas_call(
        summary_kernel,
        grid=(H // HG,),
        in_specs=[heads, heads, full((H, t)), full((H, L)), full((t, N)), full((t, N))],
        out_specs=[state, state, full((H, t)), full((H, L))],
        out_shape=[jax.ShapeDtypeStruct((H * PD, N), F32), jax.ShapeDtypeStruct((H * PD, N), F32),
                   jax.ShapeDtypeStruct((H, t), F32), jax.ShapeDtypeStruct((H, L), F32)],
        scratch_shapes=[half, half, half, half, pltpu.VMEM((H, t), F32), pltpu.VMEM((H, t + L), F32)],
        compiler_params=pltpu.CompilerParams(dimension_semantics=("arbitrary",)),
        cost_estimate=pl.CostEstimate(flops=4 * H * PD * N * t * 2, bytes_accessed=4 * H * PD * t, transcendentals=0),
        name="range_summaries",
    )(x, dy, dt, par, b, c)


def tile_sum_kernel(nd, dh_ref, out_ref, got, send, recv):
    me = lax.axis_index(AXIS)
    got[me] = jnp.transpose(jnp.concatenate([dh_ref[...], jnp.zeros((L - H, L), F32)], axis=0))[:8]
    greet_all(nd, me)
    send_all(nd, me, got, send, recv)
    wait_all(nd, me, got, send, recv)
    total = got[0]
    for d in range(1, nd):
        total = total + got[d]
    out_ref[...] = total


def tile_sum(nd, dh):
    vm = pl.BlockSpec(memory_space=pltpu.VMEM)
    return pl.pallas_call(
        functools.partial(tile_sum_kernel, nd),
        in_specs=[vm], out_specs=vm, out_shape=jax.ShapeDtypeStruct((8, L), F32),
        scratch_shapes=[pltpu.VMEM((nd, 8, L), F32), pltpu.SemaphoreType.DMA((nd,)), pltpu.SemaphoreType.DMA((nd,))],
        compiler_params=pltpu.CompilerParams(collective_id=2, has_side_effects=True),
        name="tile_sum",
    )(dh)


CH = 2
CR = CH * PD
KC = H // CH
CORE_HOP, CHIP_HOP = 2, 4
SLOTS = 2


def owner_of(nd, k):
    return jnp.where(k < nd, k, 4 * (k - nd) + 1)


def second_of(nd, me):
    return nd + (me - 1) // 4


def rows_of(k):
    return pl.ds(pl.multiple_of(k * CR, CR), CR)


def chain_kernel(nd, x_ref, dy_ref, dt_ref, cs_ref, b_ref, c_ref, tot_ref, s_ref, g_ref, s0_ref, g0_ref,
                 dui_ref, rs_ref, dg_ref, s_end, g_end, f_end,
                 gram, so_ref, go_ref, f_ref, s_out, g_out, f_out, first_sem, out_sem, s_send, s_recv, g_send, g_recv, f_send, f_recv):
    nb = x_ref.shape[2] // L
    g = pl.program_id(0)
    me = lax.axis_index(AXIS)
    last = nd - 1
    right, left = lax.rem(me + 1, nd), lax.rem(me + nd - 1, nd)

    def copy(out, into, send, recv, k, to):
        return pltpu.make_async_remote_copy(src_ref=out.at[rows_of(k)], dst_ref=into.at[rows_of(k)], send_sem=send.at[k], recv_sem=recv.at[k],
                                            device_id=(to,), device_id_type=MESH)

    def f_copy(k, slot, to):
        return pltpu.make_async_remote_copy(src_ref=f_out.at[rows_of(k)], dst_ref=f_ref.at[slot], send_sem=f_send.at[k], recv_sem=f_recv.at[slot],
                                            device_id=(to,), device_id_type=MESH)

    def combine(k, into, own_ref, out):
        for i in range(CH):
            r = pl.ds(pl.multiple_of(k * CR + i * PD, PD), PD)
            out[r] = jnp.exp2(tot_ref[pl.ds(k * CH + i, 1), :]) * into[r] + own_ref[r]

    def slot(n):
        rm = last - me
        ks = n - ((me // 2) * (CORE_HOP + CHIP_HOP) + (me % 2) * CORE_HOP)
        kg = n - ((rm // 2) * (CORE_HOP + CHIP_HOP) + (rm % 2) * CORE_HOP)

        @pl.when((ks >= 0) & (ks < KC))
        def _():
            @pl.when(me > 0)
            def _():
                copy(s_out, so_ref, s_send, s_recv, ks, right).wait_recv()

            @pl.when(me < last)
            def _():
                combine(ks, so_ref, s_ref, s_out)
                copy(s_out, so_ref, s_send, s_recv, ks, right).start()

        @pl.when((kg >= 0) & (kg < KC))
        def _():
            @pl.when(me < last)
            def _():
                copy(g_out, go_ref, g_send, g_recv, kg, left).wait_recv()

            @pl.when(me > 0)
            def _():
                combine(kg, go_ref, g_ref, g_out)
                copy(g_out, go_ref, g_send, g_recv, kg, left).start()

            @pl.when(me == 0)
            def _():
                combine(kg, go_ref, g_ref, f_out)

                @pl.when(kg == 0)
                def _():
                    f_ref[0] = f_out[rows_of(0)]

                @pl.when((kg > 0) & (kg < nd))
                def _():
                    f_copy(kg, 0, kg).start()

                @pl.when(kg >= nd)
                def _():
                    f_copy(kg, 1, 4 * (kg - nd) + 1).start()

    @pl.when(g == 0)
    def _():
        for b in range(nb):
            sl = slice(b * L, (b + 1) * L)
            gram[b] = dot(c_ref[sl, :], b_ref[sl, :], NT)
        dg_ref[...] = jnp.zeros_like(dg_ref)

        @pl.when(me == 0)
        def _():
            first = pltpu.make_async_copy(s0_ref, so_ref, first_sem)
            first.start()
            first.wait()

        @pl.when(me == last)
        def _():
            first = pltpu.make_async_copy(g0_ref, go_ref, first_sem)
            first.start()
            first.wait()

        greet_all(nd, me)

    below = lax.broadcasted_iota(jnp.int32, (L, L), 0) >= lax.broadcasted_iota(jnp.int32, (L, L), 1)
    lane = lax.broadcasted_iota(jnp.int32, (L, L), 1)

    def work(b, _):
        for p in range(SLOTS):
            slot((g * nb + b) * SLOTS + p)
        toks = pl.ds(pl.multiple_of(b * L, L), L)
        cs, dtb = cs_ref[:, toks], dt_ref[:, toks]
        cst = jnp.transpose(cs)
        gram_b = gram[b]
        dg = jnp.zeros((L, L), F32)
        rs_cols = jnp.zeros((L, L), F32)
        for j in range(HG):
            xj, dyj = x_ref[j, :, toks], dy_ref[j, :, toks]
            e = jnp.exp2(jnp.where(below, jnp.broadcast_to(cst[:, j:j + 1], (L, L)) - cs[j:j + 1], NEG))
            mhi, mlo = split(gram_b * e)
            dui_ref[j, :, toks] = dot(jnp.concatenate([dyj, dyj], axis=1), jnp.concatenate([mhi, mlo], axis=0))
            w = dot(dyj, xj, TN) * (e * dtb[j:j + 1])
            dg = dg + w
            rs = jnp.sum(w * gram_b, axis=1, keepdims=True)
            rs_cols = jnp.where(lane == j, jnp.broadcast_to(rs, (L, L)), rs_cols)
        dg_ref[b] += dg
        rs_ref[:, toks] = jnp.transpose(rs_cols)[:HG]
        return 0

    lax.fori_loop(0, nb, work, 0)

    @pl.when(g == pl.num_programs(0) - 1)
    def _():
        total = (last // 2) * (CORE_HOP + CHIP_HOP) + (last % 2) * CORE_HOP + KC

        def rest(n, _):
            slot(n)
            return 0

        lax.fori_loop((H // HG) * nb * SLOTS, total, rest, 0)

        outs = [pltpu.make_async_copy(so_ref, s_end, out_sem.at[0]), pltpu.make_async_copy(go_ref, g_end, out_sem.at[1])]
        for out in outs:
            out.start()

        def drain(k, _):
            @pl.when(me < last)
            def _():
                copy(s_out, so_ref, s_send, s_recv, k, right).wait_send()

            @pl.when(me > 0)
            def _():
                copy(g_out, go_ref, g_send, g_recv, k, left).wait_send()

            @pl.when((me == 0) & (k > 0))
            def _():
                f_copy(k, 0, last).wait_send()
            return 0

        lax.fori_loop(0, KC, drain, 0)

        @pl.when(me > 0)
        def _():
            f_copy(0, 0, 0).wait_recv()

        @pl.when(me % 4 == 1)
        def _():
            f_copy(0, 1, 0).wait_recv()

        @pl.when(me % 4 != 1)
        def _():
            f_ref[1] = jnp.zeros((CR, N), F32)

        f_end[...] = f_ref[...]
        for out in outs:
            out.wait()


def chain_and_blocks(nd, x, dy, dt, cs, b, c, tot, s_loc, g_loc, s0, g0):
    t = x.shape[2]
    nb = t // L
    full = lambda shape: pl.BlockSpec(shape, lambda g: (0,) * len(shape))
    heads = pl.BlockSpec((HG, PD, t), lambda g: (g, 0, 0))
    rows = pl.BlockSpec((HG, t), lambda g: (g, 0))
    anywhere = pl.BlockSpec(memory_space=pl.ANY)
    big = pltpu.VMEM((H * PD, N), F32)
    state = jax.ShapeDtypeStruct((H * PD, N), F32)
    return pl.pallas_call(
        functools.partial(chain_kernel, nd),
        grid=(H // HG,),
        in_specs=[heads, heads, rows, rows, full((t, N)), full((t, N)), full((H, L)), full((H * PD, N)), full((H * PD, N)), anywhere, anywhere],
        out_specs=[heads, rows, full((nb, L, L)), anywhere, anywhere, full((2, CR, N))],
        out_shape=[jax.ShapeDtypeStruct((H, PD, t), F32), jax.ShapeDtypeStruct((H, t), F32), jax.ShapeDtypeStruct((nb, L, L), F32), state, state,
                   jax.ShapeDtypeStruct((2, CR, N), F32)],
        scratch_shapes=[pltpu.VMEM((nb, L, L), F32), big, big, pltpu.VMEM((2, CR, N), F32), big, big, big, pltpu.SemaphoreType.DMA,
                        pltpu.SemaphoreType.DMA((2,))] + [pltpu.SemaphoreType.DMA((KC,))] * 5
                       + [pltpu.SemaphoreType.DMA((2,))],
        compiler_params=pltpu.CompilerParams(dimension_semantics=("arbitrary",), collective_id=0, has_side_effects=True),
        cost_estimate=pl.CostEstimate(flops=10 ** 10, bytes_accessed=10 ** 7, transcendentals=0),
        name="chain_and_blocks",
    )(x, dy, dt, cs, b, c, tot, s_loc, g_loc, s0, g0)


def carried_kernel(nd, x_ref, dy_ref, dt_ref, cs_ref, dui_ref, rs_ref, s0_ref, g1_ref, b_ref, c_ref, par_ref, dta_ref, para_ref, dg_ref, f_ref,
                   dx_ref, ddt_ref, db_ref, dc_ref, dh_ref, first_ref,
                   sf, gc, tu, sd, gh, us, db_acc, dc_acc, ec_s, td_s, tl_s, ddir_s, xd_s, dcs_s, kd_s, bb_ref, cc_ref, b2t_ref, ct_ref,
                   own_sem, f_send, f_recv):
    nb = x_ref.shape[2] // L
    g = pl.program_id(0)
    me = lax.axis_index(AXIS)
    barrier = pltpu.get_barrier_semaphore()
    has_second = me % 4 == 1

    def give(k, slot, o):
        return pltpu.make_async_remote_copy(src_ref=f_ref.at[slot], dst_ref=first_ref.at[rows_of(k)], send_sem=f_send.at[slot, o], recv_sem=f_recv.at[k],
                                            device_id=(lax.rem(me + o, nd),), device_id_type=MESH)

    def keep(k, slot):
        return pltpu.make_async_copy(f_ref.at[slot], first_ref.at[rows_of(k)], own_sem.at[slot])

    @pl.when(g == 0)
    def _():
        for o in range(1, nd):
            pl.semaphore_signal(barrier, inc=1, device_id=(lax.rem(me + o, nd),), device_id_type=MESH)
        for b in range(nb):
            bb, cc = b_ref[b * L:(b + 1) * L, :], c_ref[b * L:(b + 1) * L, :]
            bb_ref[b] = jnp.concatenate([bb, bb], axis=0)
            cc_ref[b] = jnp.concatenate([cc, cc], axis=0)
            bt = jnp.transpose(bb.astype(F32)).astype(BF16)
            b2t_ref[b] = jnp.concatenate([bt, bt], axis=0)
            ct_ref[b] = jnp.transpose(cc.astype(F32))
        db_acc[...] = jnp.zeros_like(db_acc)
        dc_acc[...] = jnp.zeros_like(dc_acc)

    @pl.when(g == 1)
    def _():
        pl.semaphore_wait(barrier, nd - 1)
        keep(me, 0).start()
        for o in range(1, nd):
            give(me, 0, o).start()

        @pl.when(has_second)
        def _():
            keep(second_of(nd, me), 1).start()
            for o in range(1, nd):
                give(second_of(nd, me), 1, o).start()

    heads = pl.ds(pl.multiple_of(g * HG, HG), HG)
    for b in range(nb):
        sl = slice(b * L, (b + 1) * L)
        cs = cs_ref[:, sl]
        tail = jnp.exp2(cs[:, L - 1:L] - cs)
        ec_s[b] = jnp.exp2(cs)
        tl_s[b] = tail
        td_s[b] = tail * dt_ref[:, sl]

    sf[0] = s0_ref[...]

    def forward(b, _):
        toks = pl.ds(pl.multiple_of(b * L, L), L)
        etot = ec_s[b][:, L - 1:L]
        td = td_s[b]
        for j in range(HG):
            hi, lo = split(x_ref[j, :, toks].astype(F32) * td[j:j + 1])
            tu[b, j * PD:(j + 1) * PD, :L] = hi
            tu[b, j * PD:(j + 1) * PD, L:] = lo
        new = dot(tu[b], bb_ref[b])
        for j in range(HG):
            pr = slice(j * PD, (j + 1) * PD)
            sf[b + 1, pr] = etot[j:j + 1] * sf[b, pr] + new[pr]
        return 0

    lax.fori_loop(0, nb, forward, 0)
    gc[...] = g1_ref[...]

    def backward(i, _):
        b = nb - 1 - i
        toks = pl.ds(pl.multiple_of(b * L, L), L)
        ec, tl, dtb = ec_s[b], tl_s[b], dt_ref[:, toks]
        etot = ec[:, L - 1:L]
        kd = []
        for j in range(HG):
            pr = slice(j * PD, (j + 1) * PD)
            gj = gc[pr]
            kd.append(jnp.sum(gj * sf[b + 1, pr], axis=0, keepdims=True))
            hi, lo = split(gj)
            gh[pr, :L] = hi
            gh[pr, L:] = lo
            hi, lo = split(dy_ref[j, :, toks].astype(F32) * ec[j:j + 1])
            sd[pr, :L] = hi
            sd[pr, L:] = lo
        kd_s[b, heads] = jnp.concatenate(kd, axis=0)
        us[...] = dot(gh[...], b2t_ref[b])
        db_acc[b] += (dot(gh[:, :L], tu[b, :, :L], TN) + dot(gh[:, L:], tu[b, :, :L], TN)) + dot(gh[:, :L], tu[b, :, L:], TN)
        ct = ct_ref[b]
        dc = jnp.zeros((N, L), F32)
        ddir, xd, inter = [], [], []
        for j in range(HG):
            pr = slice(j * PD, (j + 1) * PD)
            du = dui_ref[j, :, toks] + us[pr] * tl[j:j + 1]
            xf, dyf = x_ref[j, :, toks].astype(F32), dy_ref[j, :, toks].astype(F32)
            ddir.append(jnp.sum(du * xf, axis=0, keepdims=True))
            xd.append(jnp.sum(dyf * xf, axis=0, keepdims=True))
            dx_ref[j, :, toks] = (du * dtb[j:j + 1] + dyf * par_ref[j:j + 1, 1:2]).astype(BF16)
            shi, slo = split(sf[b, pr])
            st = jnp.transpose(jnp.concatenate([shi, slo, shi, slo], axis=0))
            dhi, dlo = sd[pr, :L], sd[pr, L:]
            z = dot(st, jnp.concatenate([dhi, dhi, dlo, dlo], axis=0))
            dc = dc + z
            inter.append(jnp.sum(z * ct, axis=0, keepdims=True))
        dc_acc[b] += dc
        ddir = jnp.concatenate(ddir, axis=0)
        ddir_s[b, heads] = ddir
        xd_s[b, heads] = jnp.concatenate(xd, axis=0)
        dcs_s[b, heads] = rs_ref[:, toks] + jnp.concatenate(inter, axis=0) - ddir * dtb
        grow = dot(sd[...], cc_ref[b])
        for j in range(HG):
            pr = slice(j * PD, (j + 1) * PD)
            gc[pr] = etot[j:j + 1] * gc[pr] + grow[pr]
        return 0

    lax.fori_loop(0, nb, backward, 0)

    @pl.when(g == pl.num_programs(0) - 1)
    def _():
        after = (lax.broadcasted_iota(jnp.int32, (L, L), 0) >= lax.broadcasted_iota(jnp.int32, (L, L), 1)).astype(F32)
        da_sum = jnp.zeros((H, 1), F32)
        dd_sum = jnp.zeros((H, 1), F32)
        for b in range(nb):
            sl = slice(b * L, (b + 1) * L)
            da = dot(dcs_s[b], after, precision=HIGHEST) + jnp.sum(kd_s[b], axis=1, keepdims=True)
            dta = da * para_ref[:, 0:1]
            ddt_ref[:, sl] = ddir_s[b] + dta
            da_sum += jnp.sum(dta * dta_ref[:, sl], axis=1, keepdims=True)
            dd_sum += jnp.sum(xd_s[b], axis=1, keepdims=True)
            ghi, glo = split(dg_ref[b])
            dbt = jnp.transpose(db_acc[b]) + (dot(ghi, cc_ref[b, :L, :], TN) + dot(glo, cc_ref[b, :L, :], TN))
            dct = jnp.transpose(dc_acc[b]) + (dot(ghi, bb_ref[b, :L, :]) + dot(glo, bb_ref[b, :L, :]))
            db_ref[sl, :] = dbt.astype(BF16)
            dc_ref[sl, :] = dct.astype(BF16)
        lane_h = lax.broadcasted_iota(jnp.int32, (H, L), 1)
        dh_ref[...] = jnp.where(lane_h == 0, da_sum, jnp.where(lane_h == 1, dd_sum, 0.0))
        keep(me, 0).wait()
        for o in range(1, nd):
            give(me, 0, o).wait_send()

        @pl.when(has_second)
        def _():
            keep(second_of(nd, me), 1).wait()
            for o in range(1, nd):
                give(second_of(nd, me), 1, o).wait_send()

        for k in range(KC):
            @pl.when(me != (k if k < nd else 4 * (k - nd) + 1))
            def _():
                give(k, 0, 1).wait_recv()


def carried(nd, x, dy, dt, cs, dui, rs, s_start, ds_end, b, c, par, dg, f):
    t = x.shape[2]
    nb = t // L
    full = lambda shape: pl.BlockSpec(shape, lambda g: (0,) * len(shape))
    heads = pl.BlockSpec((HG, PD, t), lambda g: (g, 0, 0))
    rows = pl.BlockSpec((HG, t), lambda g: (g, 0))
    state = pl.BlockSpec((HG * PD, N), lambda g: (g, 0))
    one = pl.BlockSpec((HG, L), lambda g: (g, 0))
    vm = lambda shape, dtype=F32: pltpu.VMEM(shape, dtype)
    return pl.pallas_call(
        functools.partial(carried_kernel, nd),
        grid=(H // HG,),
        in_specs=[heads, heads, rows, rows, heads, rows, state, state, full((t, N)), full((t, N)), one, full((H, t)), full((H, L)),
                  full((nb, L, L)), full((2, CR, N))],
        out_specs=[heads, full((H, t)), full((t, N)), full((t, N)), full((H, L)), pl.BlockSpec(memory_space=pl.ANY)],
        out_shape=[jax.ShapeDtypeStruct((H, PD, t), BF16), jax.ShapeDtypeStruct((H, t), F32), jax.ShapeDtypeStruct((t, N), BF16),
                   jax.ShapeDtypeStruct((t, N), BF16), jax.ShapeDtypeStruct((H, L), F32), jax.ShapeDtypeStruct((H * PD, N), F32)],
        scratch_shapes=[vm((nb + 1, HG * PD, N)), vm((HG * PD, N)), vm((nb, HG * PD, 2 * L), BF16), vm((HG * PD, 2 * L), BF16),
                        vm((HG * PD, 2 * N), BF16), vm((HG * PD, L)), vm((nb, N, L)), vm((nb, N, L)),
                        vm((nb, HG, L)), vm((nb, HG, L)), vm((nb, HG, L)), vm((nb, H, L)), vm((nb, H, L)), vm((nb, H, L)), vm((nb, H, N)),
                        vm((nb, 2 * L, N), BF16), vm((nb, 2 * L, N), BF16), vm((nb, 2 * N, L), BF16), vm((nb, N, L)),
                        pltpu.SemaphoreType.DMA((2,)), pltpu.SemaphoreType.DMA((2, nd)), pltpu.SemaphoreType.DMA((KC,))],
        compiler_params=pltpu.CompilerParams(dimension_semantics=("arbitrary",), collective_id=1, has_side_effects=True),
        cost_estimate=pl.CostEstimate(flops=5 * 10 ** 10, bytes_accessed=6 * H * PD * t, transcendentals=H * t * L),
        name="carried_backward",
    )(x, dy, dt, cs, dui, rs, s_start, ds_end, b, c, par, dt, par, dg, f)


def solution(mesh):
    nd = mesh.shape[AXIS]
    tok4 = P(None, AXIS, None, None)
    tok3 = P(None, AXIS, None)

    def device_step(x_loc, dt_loc, a_log, b_loc, c_loc, d_skip, s_init, dy_loc, ds_last):
        x, dy = jnp.transpose(x_loc[0], (1, 2, 0)), jnp.transpose(dy_loc[0], (1, 2, 0))
        dt = jnp.transpose(dt_loc[0])
        b, c = b_loc[0], c_loc[0]
        col = jnp.arange(L)[None, :]
        par = jnp.where(col == 0, -jnp.exp(a_log)[:, None], jnp.where(col == 1, d_skip[:, None], 0.0))
        s_loc, g_loc, cs, tot = summaries(x, dy, dt, par, b, c)
        s0, g0 = s_init.reshape(H * PD, N), ds_last.reshape(H * PD, N)
        dui, rs, dg, s_start, ds_end, f = chain_and_blocks(nd, x, dy, dt, cs, b, c, tot, s_loc, g_loc, s0, g0)
        dx, ddt, db, dc, dh, first = carried(nd, x, dy, dt, cs, dui, rs, s_start, ds_end, b, c, par, dg, f)
        dh = tile_sum(nd, dh)
        return (jnp.transpose(dx, (2, 0, 1))[None], jnp.transpose(ddt)[None], db[None], dc[None], first.reshape(1, H, PD, N), dh[0, :H], dh[1, :H])

    return jax.shard_map(device_step, mesh=mesh,
                         in_specs=(tok4, tok3, P(), tok3, tok3, P(), P(), tok4, P()),
                         out_specs=(tok4, tok3, tok3, tok3, P(), P(), P()),
                         check_vma=False)
```

time: 306 us -> 261 us (0.85)
  Pallas kernels: 280 us -> 245 us
  between operations: 14.1 us -> 0.67 us
  local copies, waits for them, and re-layouts: 1.28 us -> 12.4 us
  other arithmetic: 10.1 us -> 2.03 us
    pallas_call x3, Pallas kernels: 269 us -> 225 us  [the longest x1 137 us: chain_and_blocks(): pl.pallas_call(functools.partial(chain_kernel, nd), grid=(H // HG,), in_s...]
    unnamed x2 -> x13, local copies, waits for them, and re-layouts: 0.01 us -> 11.1 us
    pallas_call x1, Pallas kernels: 10.9 us -> 19.8 us  [tile_sum(): pl.pallas_call(functools.partial(tile_sum_kernel, nd), in_specs=[vm], out...]
    broadcast_in_dim x1 -> x0, other arithmetic: 3.55 us -> none  [device_step(): ds_first[None]]
    mul x1 -> x0, other arithmetic: 3.47 us -> none  [device_step(): part = jnp.exp2(before)[:, None, None] * g_loc.reshape(H, PD, N)]
  transfers between devices with their start and end apart: 1 -> 0, of which waited for: 0 -> 0; matrix products, arithmetic and copies ran while one was open for 0% -> 0% of each run, Pallas kernels for 83% -> 0%
where the time goes in v2:
time: 261 us; the launch traced here: 260 us
  Pallas kernels  245 us (94%)
  local copies, waits for them, and re-layouts  12.4 us (5%)
    pallas_call x1, Pallas kernels, chain_and_blocks(): pl.pallas_call(functools.partial(chain_kernel, nd), grid=(H // HG,), in_s...  137 us
    pallas_call x1, Pallas kernels, carried(): pl.pallas_call(functools.partial(carried_kernel, nd), grid=(H // HG,), in...  70.5 us
    pallas_call x1, Pallas kernels, tile_sum(): pl.pallas_call(functools.partial(tile_sum_kernel, nd), in_specs=[vm], out...  19.8 us
    pallas_call x1, Pallas kernels, summaries(): pl.pallas_call(summary_kernel, grid=(H // HG,), in_specs=[heads, heads, f...  17.6 us
    unnamed x13, local copies, waits for them, and re-layouts  11.1 us

profile of v2, /device:TPU:0, one launch (start us, length us, event | category | flops | bytes accessed | tf_op | source)
XLA Modules:
  0.0 260.0 jit_solution(114991841780840528)
XLA Ops:
  0.6 0.7 exponential_negate_fusion
  1.3 1.4 select_select_fusion.par_ref.para_ref
  2.7 17.6 %range_summaries.1 = (f32[5120,128]{1,0:T(8,128)}, f32[5120,128]{1,0:T(8,128)}, f32[80,768]{1,0:T(8,128)}, f32[80,128]{1,0:T(8,128)}) custom-call(bf16[80,64,768]{2,1,0:T(8,128)(2,1)} %bitcast.26, bf16[80,64,768]{2,1,0:T(8,128)(2,1)} %bitcast.29, f32[80,768]{1,0:T(8,128)} %bitcast.35, f32[80,128]{1,0:T(8,128)} %select_select_fusion.par_ref.para_ref, ...), custom_call_target="tpu_custom_call" | custom-call | flops 4026531840 | bytes 15728640 | tf_op jit(solution)/shard_map/range_summaries/pallas_call | solution.py:99
  20.3 137.0 %chain_and_blocks.1 = (f32[80,64,768]{2,1,0:T(8,128)}, f32[80,768]{1,0:T(8,128)}, f32[6,128,128]{2,1,0:T(8,128)}, f32[5120,128]{1,0:T(8,128)}, f32[5120,128]{1,0:T(8,128)}, /*index=5*/f32[2,128,128]{2,1,0:T(8,128)}) custom-call(bf16[80,64,768]{2,1,0:T(8,128)(2,1)} %bitcast.27, bf16[80,64,768]{2,1,0:T(8,128)(2,1)} %bitcast.30, f32[80,768]{1,0:T(8,128)} %bitcast.36, ...), custom_call_target="tpu_custom_call" | custom-call | flops 10000000000 | bytes 10000000 | tf_op jit(solution)/shard_map/chain_and_blocks/pallas_call | solution.py:324
  157.3 70.5 %carried_backward.1 = (bf16[80,64,768]{2,1,0:T(8,128)(2,1)}, f32[80,768]{1,0:T(8,128)}, bf16[768,128]{1,0:T(8,128)(2,1)}, bf16[768,128]{1,0:T(8,128)(2,1)}, f32[80,128]{1,0:T(8,128)}, /*index=5*/f32[5120,128]{1,0:T(8,128)}) custom-call(bf16[80,64,768]{2,1,0:T(8,128)(2,1)} %bitcast.28, bf16[80,64,768]{2,1,0:T(8,128)(2,1)} %bitcast.31, f32[80,768]{1,0:T(8,128)} %bitcast.37, ...), custom_call_target="tpu_custom_call" | custom-call | flops 49999998976 | bytes 23592960 | tf_op jit(solution)/shard_map/carried_backward/pallas_call | solution.py:504
  227.8 19.8 %tile_sum.1 = f32[8,128]{1,0:T(8,128)} custom-call(f32[80,128]{1,0:T(8,128)} %get-tuple-element.38.dh_ref), custom_call_target="tpu_custom_call" | custom-call | tf_op jit(solution)/shard_map/tile_sum/pallas_call | solution.py:127
  247.6 1.3 slice_bitcast_fusion
  248.9 0.0 copy-start.1
  248.9 0.0 copy-start.3
  248.9 0.0 copy-start.2
  248.9 0.0 copy-start
  248.9 7.6 %copy.21 = bf16[1,768,80,64]{1,3,2,0:T(8,128)(2,1)} copy(bf16[1,768,80,64]{1,3,2,0:T(8,128)(2,1)} %bitcast.32) | data formatting | bytes 15728640
  256.5 0.0 copy-done.1
  256.5 0.7 copy.22
  257.2 0.0 copy-done.3
  257.2 0.7 copy.23
  257.9 0.0 copy-done.2
  257.9 0.7 copy.24
  258.6 0.0 copy-done
  258.6 1.5 copy.25
  (1 shorter events, 0.0 us)
Async XLA Ops:
  248.9 7.6 %copy-start.1 = (f32[80,768]{1,0:T(8,128)S(1)}, f32[80,768]{1,0:T(8,128)}, u32[]{:S(2)}) copy-start(f32[80,768]{1,0:T(8,128)} %get-tuple-element.34) | copy-start | bytes 737284
  248.9 8.3 %copy-start.3 = (bf16[768,128]{1,0:T(8,128)(2,1)S(1)}, bf16[768,128]{1,0:T(8,128)(2,1)}, u32[]{:S(2)}) copy-start(bf16[768,128]{1,0:T(8,128)(2,1)} %get-tuple-element.35) | copy-start | bytes 589828
  248.9 9.0 %copy-start.2 = (bf16[768,128]{1,0:T(8,128)(2,1)S(1)}, bf16[768,128]{1,0:T(8,128)(2,1)}, u32[]{:S(2)}) copy-start(bf16[768,128]{1,0:T(8,128)(2,1)} %get-tuple-element.36) | copy-start | bytes 589828
  248.9 9.7 %copy-start = (f32[5120,128]{1,0:T(8,128)S(1)}, f32[5120,128]{1,0:T(8,128)}, u32[]{:S(2)}) copy-start(f32[5120,128]{1,0:T(8,128)} %get-tuple-element.37) | copy-start | bytes 7864324

commit v3 on v2

--- a/solution.py
+++ b/solution.py
@@ -133,117 +133,169 @@
     )(dh)
 
 
-CH = 2
-CR = CH * PD
-KC = H // CH
-CORE_HOP, CHIP_HOP = 2, 4
-SLOTS = 2
-
-
-def owner_of(nd, k):
-    return jnp.where(k < nd, k, 4 * (k - nd) + 1)
-
-
-def second_of(nd, me):
-    return nd + (me - 1) // 4
-
-
-def rows_of(k):
-    return pl.ds(pl.multiple_of(k * CR, CR), CR)
-
-
-def chain_kernel(nd, x_ref, dy_ref, dt_ref, cs_ref, b_ref, c_ref, tot_ref, s_ref, g_ref, s0_ref, g0_ref,
-                 dui_ref, rs_ref, dg_ref, s_end, g_end, f_end,
-                 gram, so_ref, go_ref, f_ref, s_out, g_out, f_out, first_sem, out_sem, s_send, s_recv, g_send, g_recv, f_send, f_recv):
+GD = 4
+QH = H // GD
+QR = QH * PD
+HOP = 3
+BACK = 3
+
+
+def chain_kernel(nd, x_ref, dy_ref, dt_ref, cs_ref, b_ref, c_ref, tot_ref, s_hbm, g_hbm, s0_ref, g0_ref,
+                 dui_ref, rs_ref, dg_ref, s_end, g_end, f_ref,
+                 gram, tots, own, par, tq, tx, xin, cin, cout, bsend, brecv, dsend, into, local_sem, tot_send, tot_recv, par_send, par_recv,
+                 x_send, x_recv, c_send, c_recv, b_send, b_recv, d_send, d_recv, out_sem):
     nb = x_ref.shape[2] // L
+    ng = nd // GD
     g = pl.program_id(0)
     me = lax.axis_index(AXIS)
-    last = nd - 1
-    right, left = lax.rem(me + 1, nd), lax.rem(me + nd - 1, nd)
-
-    def copy(out, into, send, recv, k, to):
-        return pltpu.make_async_remote_copy(src_ref=out.at[rows_of(k)], dst_ref=into.at[rows_of(k)], send_sem=send.at[k], recv_sem=recv.at[k],
-                                            device_id=(to,), device_id_type=MESH)
-
-    def f_copy(k, slot, to):
-        return pltpu.make_async_remote_copy(src_ref=f_out.at[rows_of(k)], dst_ref=f_ref.at[slot], send_sem=f_send.at[k], recv_sem=f_recv.at[slot],
-                                            device_id=(to,), device_id_type=MESH)
-
-    def combine(k, into, own_ref, out):
-        for i in range(CH):
-            r = pl.ds(pl.multiple_of(k * CR + i * PD, PD), PD)
-            out[r] = jnp.exp2(tot_ref[pl.ds(k * CH + i, 1), :]) * into[r] + own_ref[r]
+    q, core, chip, pos = lax.rem(me, 4), lax.rem(me, 2), lax.rem(me // 2, 2), me // 4
+    other_core, other_chip = me + 1 - 2 * core, me + 2 - 4 * chip
+    oq = lax.rem(q + 2, 4)
+    local = (s_hbm, g_hbm)
+
+    def rows(head, n=1):
+        return pl.ds(pl.multiple_of(head * PD, PD), n * PD)
+
+    def remote(src, dst, send, recv, to):
+        return pltpu.make_async_remote_copy(src_ref=src, dst_ref=dst, send_sem=send, recv_sem=recv, device_id=(to,), device_id_type=MESH)
+
+    def tot_copy(o):
+        return remote(tot_ref, tots.at[q], tot_send.at[o], tot_recv.at[o], 4 * pos + lax.rem(q + o, 4))
+
+    def tot_got(o):
+        src = lax.rem(q + 4 - o, 4)
+        return remote(tot_ref, tots.at[src], tot_send.at[o], tot_recv.at[o], 4 * pos + src)
+
+    def par_copy(d, i):
+        return remote(local[d].at[rows(QH * (2 * i + 1 - core), QH)], par.at[d, i], par_send.at[d, i], par_recv.at[d, i], other_core)
+
+    def x_copy(d, k):
+        return remote(tx.at[d, rows(k)], xin.at[d, rows(k)], x_send.at[d, k], x_recv.at[d, k], other_chip)
+
+    def c_copy(d, k):
+        return remote(cout.at[d, rows(k)], cin.at[d, rows(k)], c_send.at[d, k], c_recv.at[d, k], me + (4 - 8 * d))
+
+    def b_copy(d, k):
+        return remote(bsend.at[d, rows(k)], brecv.at[d, rows(k)], b_send.at[d, k], b_recv.at[d, k], other_chip)
+
+    def d_copy(d, i, k):
+        head = QH * (2 * i + core) + k
+        return remote(dsend.at[d, i, rows(k)], into.at[d, rows(head)], d_send.at[d, i, k], d_recv.at[d, i, k], other_core)
+
+    def decay(qq, head):
+        return tots[qq, pl.ds(head, 1), :]
+
+    def core_level(d, i, k, state):
+        head = QH * (2 * i + core) + k
+        mine_near = core == d
+        near = jnp.where(mine_near, own[d, rows(head)], par[d, i, rows(k)])
+        e_near = jnp.exp2(decay(2 * chip + d, head))
+        far = e_near * state + near
+        into[d, rows(head)] = jnp.where(mine_near, state, far)
+        dsend[d, i, rows(k)] = jnp.where(mine_near, far, state)
+        d_copy(d, i, k).start()
+
+    def chain_step(d, k):
+        head = QH * q + k
+        has_prev = (pos > 0) if d == 0 else (pos < ng - 1)
+        has_next = (pos < ng - 1) if d == 0 else (pos > 0)
+        x_copy(d, k).wait_recv()
+
+        @pl.when(has_prev)
+        def _():
+            c_copy(d, k).wait_recv()
+
+        mine_near = chip == d
+        state = cin[d, rows(k)]
+        near = jnp.where(mine_near, tq[d, rows(k)], xin[d, rows(k)])
+        afar = jnp.where(mine_near, xin[d, rows(k)], tq[d, rows(k)])
+        e_near = jnp.exp2(decay(2 * d, head) + decay(2 * d + 1, head))
+        e_far = jnp.exp2(decay(2 - 2 * d, head) + decay(3 - 2 * d, head))
+        far = e_near * state + near
+        cout[d, rows(k)] = e_far * far + afar
+
+        @pl.when(has_next)
+        def _():
+            c_copy(d, k).start()
+
+        bsend[d, rows(k)] = jnp.where(mine_near, far, state)
+        b_copy(d, k).start()
+        core_level(d, chip, k, jnp.where(mine_near, state, far))
+
+    def back_step(d, k):
+        b_copy(d, k).wait_recv()
+        core_level(d, 1 - chip, k, brecv[d, rows(k)])
 
     def slot(n):
-        rm = last - me
-        ks = n - ((me // 2) * (CORE_HOP + CHIP_HOP) + (me % 2) * CORE_HOP)
-        kg = n - ((rm // 2) * (CORE_HOP + CHIP_HOP) + (rm % 2) * CORE_HOP)
-
-        @pl.when((ks >= 0) & (ks < KC))
-        def _():
-            @pl.when(me > 0)
+        for d in range(2):
+            k = n - HOP * (pos if d == 0 else ng - 1 - pos)
+
+            @pl.when((k >= 0) & (k < QH))
             def _():
-                copy(s_out, so_ref, s_send, s_recv, ks, right).wait_recv()
-
-            @pl.when(me < last)
+                chain_step(d, k)
+
+            @pl.when((k >= BACK) & (k < QH + BACK))
             def _():
-                combine(ks, so_ref, s_ref, s_out)
-                copy(s_out, so_ref, s_send, s_recv, ks, right).start()
-
-        @pl.when((kg >= 0) & (kg < KC))
-        def _():
-            @pl.when(me < last)
-            def _():
-                copy(g_out, go_ref, g_send, g_recv, kg, left).wait_recv()
-
-            @pl.when(me > 0)
-            def _():
-                combine(kg, go_ref, g_ref, g_out)
-                copy(g_out, go_ref, g_send, g_recv, kg, left).start()
-
-            @pl.when(me == 0)
-            def _():
-                combine(kg, go_ref, g_ref, f_out)
-
-                @pl.when(kg == 0)
-                def _():
-                    f_ref[0] = f_out[rows_of(0)]
-
-                @pl.when((kg > 0) & (kg < nd))
-                def _():
-                    f_copy(kg, 0, kg).start()
-
-                @pl.when(kg >= nd)
-                def _():
-                    f_copy(kg, 1, 4 * (kg - nd) + 1).start()
+                back_step(d, k - BACK)
 
     @pl.when(g == 0)
     def _():
+        locals_ = [pltpu.make_async_copy(s_hbm, own.at[0], local_sem.at[0]), pltpu.make_async_copy(g_hbm, own.at[1], local_sem.at[1]),
+                   pltpu.make_async_copy(tot_ref, tots.at[q], local_sem.at[2]),
+                   pltpu.make_async_copy(s0_ref.at[rows(QH * q, QH)], cin.at[0], local_sem.at[3]),
+                   pltpu.make_async_copy(g0_ref.at[rows(QH * q, QH)], cin.at[1], local_sem.at[4])]
+        for cp in locals_[:3]:
+            cp.start()
+
+        @pl.when(pos == 0)
+        def _():
+            locals_[3].start()
+            locals_[3].wait()
+
+        @pl.when(pos == ng - 1)
+        def _():
+            locals_[4].start()
+            locals_[4].wait()
+
+        greet_all(nd, me)
+        for o in range(1, GD):
+            tot_copy(o).start()
+        for d in range(2):
+            for i in range(2):
+                par_copy(d, i).start()
         for b in range(nb):
             sl = slice(b * L, (b + 1) * L)
             gram[b] = dot(c_ref[sl, :], b_ref[sl, :], NT)
         dg_ref[...] = jnp.zeros_like(dg_ref)
-
-        @pl.when(me == 0)
-        def _():
-            first = pltpu.make_async_copy(s0_ref, so_ref, first_sem)
-            first.start()
-            first.wait()
-
-        @pl.when(me == last)
-        def _():
-            first = pltpu.make_async_copy(g0_ref, go_ref, first_sem)
-            first.start()
-            first.wait()
-
-        greet_all(nd, me)
+        for cp in locals_[:3]:
+            cp.wait()
+        for o in range(1, GD):
+            tot_got(o).wait_recv()
+        for d in range(2):
+            for i in range(2):
+                par_copy(d, i).wait_recv()
+
+        def combine(d, i, k):
+            head = QH * (2 * i + core) + k
+            mine_near = core == d
+            mine, his = own[d, rows(head)], par[d, i, rows(k)]
+            e_far = jnp.exp2(decay(2 * chip + 1 - d, head))
+            return e_far * jnp.where(mine_near, mine, his) + jnp.where(mine_near, his, mine)
+
+        def front(k, _):
+            for d in range(2):
+                tx[d, rows(k)] = combine(d, 1 - chip, k)
+                x_copy(d, k).start()
+                tq[d, rows(k)] = combine(d, chip, k)
+            return 0
+
+        lax.fori_loop(0, QH, front, 0)
 
     below = lax.broadcasted_iota(jnp.int32, (L, L), 0) >= lax.broadcasted_iota(jnp.int32, (L, L), 1)
     lane = lax.broadcasted_iota(jnp.int32, (L, L), 1)
 
     def work(b, _):
-        for p in range(SLOTS):
-            slot((g * nb + b) * SLOTS + p)
+        slot(g * nb + b)
         toks = pl.ds(pl.multiple_of(b * L, L), L)
         cs, dtb = cs_ref[:, toks], dt_ref[:, toks]
         cst = jnp.transpose(cs)
@@ -267,47 +319,35 @@
 
     @pl.when(g == pl.num_programs(0) - 1)
     def _():
-        total = (last // 2) * (CORE_HOP + CHIP_HOP) + (last % 2) * CORE_HOP + KC
-
         def rest(n, _):
             slot(n)
             return 0
 
-        lax.fori_loop((H // HG) * nb * SLOTS, total, rest, 0)
-
-        outs = [pltpu.make_async_copy(so_ref, s_end, out_sem.at[0]), pltpu.make_async_copy(go_ref, g_end, out_sem.at[1])]
+        lax.fori_loop((H // HG) * nb, HOP * (ng - 1) + QH + BACK, rest, 0)
+
+        def drain(k, _):
+            for d in range(2):
+                x_copy(d, k).wait_send()
+                b_copy(d, k).wait_send()
+
+                @pl.when((pos < ng - 1) if d == 0 else (pos > 0))
+                def _():
+                    c_copy(d, k).wait_send()
+
+                for i in range(2):
+                    d_copy(d, i, k).wait()
+            return 0
+
+        lax.fori_loop(0, QH, drain, 0)
+        outs = [pltpu.make_async_copy(into.at[0], s_end, out_sem.at[0]), pltpu.make_async_copy(into.at[1], g_end, out_sem.at[1])]
         for out in outs:
             out.start()
-
-        def drain(k, _):
-            @pl.when(me < last)
-            def _():
-                copy(s_out, so_ref, s_send, s_recv, k, right).wait_send()
-
-            @pl.when(me > 0)
-            def _():
-                copy(g_out, go_ref, g_send, g_recv, k, left).wait_send()
-
-            @pl.when((me == 0) & (k > 0))
-            def _():
-                f_copy(k, 0, last).wait_send()
-            return 0
-
-        lax.fori_loop(0, KC, drain, 0)
-
-        @pl.when(me > 0)
-        def _():
-            f_copy(0, 0, 0).wait_recv()
-
-        @pl.when(me % 4 == 1)
-        def _():
-            f_copy(0, 1, 0).wait_recv()
-
-        @pl.when(me % 4 != 1)
-        def _():
-            f_ref[1] = jnp.zeros((CR, N), F32)
-
-        f_end[...] = f_ref[...]
+        for o in range(1, GD):
+            tot_copy(o).wait_send()
+        for d in range(2):
+            for i in range(2):
+                par_copy(d, i).wait_send()
+        f_ref[...] = cout[1]
         for out in outs:
             out.wait()
 
@@ -319,40 +359,73 @@
     heads = pl.BlockSpec((HG, PD, t), lambda g: (g, 0, 0))
     rows = pl.BlockSpec((HG, t), lambda g: (g, 0))
     anywhere = pl.BlockSpec(memory_space=pl.ANY)
-    big = pltpu.VMEM((H * PD, N), F32)
+    quarter = pltpu.VMEM((2, QR, N), F32)
+    whole = pltpu.VMEM((2, H * PD, N), F32)
+    halves = pltpu.VMEM((2, 2, QR, N), F32)
+    sems = lambda *shape: pltpu.SemaphoreType.DMA(shape)
     state = jax.ShapeDtypeStruct((H * PD, N), F32)
     return pl.pallas_call(
         functools.partial(chain_kernel, nd),
         grid=(H // HG,),
-        in_specs=[heads, heads, rows, rows, full((t, N)), full((t, N)), full((H, L)), full((H * PD, N)), full((H * PD, N)), anywhere, anywhere],
-        out_specs=[heads, rows, full((nb, L, L)), anywhere, anywhere, full((2, CR, N))],
+        in_specs=[heads, heads, rows, rows, full((t, N)), full((t, N))] + [anywhere] * 5,
+        out_specs=[heads, rows, full((nb, L, L)), anywhere, anywhere, full((QR, N))],
         out_shape=[jax.ShapeDtypeStruct((H, PD, t), F32), jax.ShapeDtypeStruct((H, t), F32), jax.ShapeDtypeStruct((nb, L, L), F32), state, state,
-                   jax.ShapeDtypeStruct((2, CR, N), F32)],
-        scratch_shapes=[pltpu.VMEM((nb, L, L), F32), big, big, pltpu.VMEM((2, CR, N), F32), big, big, big, pltpu.SemaphoreType.DMA,
-                        pltpu.SemaphoreType.DMA((2,))] + [pltpu.SemaphoreType.DMA((KC,))] * 5
-                       + [pltpu.SemaphoreType.DMA((2,))],
+                   jax.ShapeDtypeStruct((QR, N), F32)],
+        scratch_shapes=[pltpu.VMEM((nb, L, L), F32), pltpu.VMEM((GD, H, L), F32), whole, halves] + [quarter] * 7 + [halves, whole]
+                       + [sems(5), sems(GD), sems(GD), sems(2, 2), sems(2, 2)] + [sems(2, QH)] * 6 + [sems(2, 2, QH)] * 2 + [sems(2)],
         compiler_params=pltpu.CompilerParams(dimension_semantics=("arbitrary",), collective_id=0, has_side_effects=True),
         cost_estimate=pl.CostEstimate(flops=10 ** 10, bytes_accessed=10 ** 7, transcendentals=0),
         name="chain_and_blocks",
     )(x, dy, dt, cs, b, c, tot, s_loc, g_loc, s0, g0)
 
 
+FC = 5
+FR = QR // FC
+F_HOP = 5
+
+
 def carried_kernel(nd, x_ref, dy_ref, dt_ref, cs_ref, dui_ref, rs_ref, s0_ref, g1_ref, b_ref, c_ref, par_ref, dta_ref, para_ref, dg_ref, f_ref,
                    dx_ref, ddt_ref, db_ref, dc_ref, dh_ref, first_ref,
                    sf, gc, tu, sd, gh, us, db_acc, dc_acc, ec_s, td_s, tl_s, ddir_s, xd_s, dcs_s, kd_s, bb_ref, cc_ref, b2t_ref, ct_ref,
-                   own_sem, f_send, f_recv):
+                   fq, own_sem, f_send, f_recv, p_send, p_recv):
     nb = x_ref.shape[2] // L
     g = pl.program_id(0)
     me = lax.axis_index(AXIS)
     barrier = pltpu.get_barrier_semaphore()
-    has_second = me % 4 == 1
-
-    def give(k, slot, o):
-        return pltpu.make_async_remote_copy(src_ref=f_ref.at[slot], dst_ref=first_ref.at[rows_of(k)], send_sem=f_send.at[slot, o], recv_sem=f_recv.at[k],
-                                            device_id=(lax.rem(me + o, nd),), device_id_type=MESH)
-
-    def keep(k, slot):
-        return pltpu.make_async_copy(f_ref.at[slot], first_ref.at[rows_of(k)], own_sem.at[slot])
+    ng = nd // GD
+    q, pos = lax.rem(me, 4), me // 4
+
+    def part(k):
+        return pl.ds(pl.multiple_of(k * FR, FR), FR)
+
+    def remote(src, dst, send, recv, to):
+        return pltpu.make_async_remote_copy(src_ref=src, dst_ref=dst, send_sem=send, recv_sem=recv, device_id=(to,), device_id_type=MESH)
+
+    def f_copy(k):
+        return remote(fq.at[part(k)], fq.at[part(k)], f_send.at[k], f_recv.at[k], me + 4)
+
+    def give(o, k):
+        return remote(fq.at[part(k)], first_ref.at[part(q * FC + k)], p_send.at[o, k], p_recv.at[o, k], 4 * pos + lax.rem(q + o, 4))
+
+    def given(o, k):
+        src = lax.rem(q + 4 - o, 4)
+        return remote(fq.at[part(k)], first_ref.at[part(src * FC + k)], p_send.at[o, k], p_recv.at[o, k], 4 * pos + src)
+
+    def keep(k):
+        return pltpu.make_async_copy(fq.at[part(k)], first_ref.at[part(q * FC + k)], own_sem.at[k])
+
+    def first_step(k):
+        @pl.when(pos > 0)
+        def _():
+            f_copy(k).wait_recv()
+
+        @pl.when(pos < ng - 1)
+        def _():
+            f_copy(k).start()
+
+        keep(k).start()
+        for o in range(1, GD):
+            give(o, k).start()
 
     @pl.when(g == 0)
     def _():
@@ -371,15 +444,10 @@
     @pl.when(g == 1)
     def _():
         pl.semaphore_wait(barrier, nd - 1)
-        keep(me, 0).start()
-        for o in range(1, nd):
-            give(me, 0, o).start()
-
-        @pl.when(has_second)
-        def _():
-            keep(second_of(nd, me), 1).start()
-            for o in range(1, nd):
-                give(second_of(nd, me), 1, o).start()
+
+        @pl.when(pos == 0)
+        def _():
+            fq[...] = f_ref[...]
 
     heads = pl.ds(pl.multiple_of(g * HG, HG), HG)
     for b in range(nb):
@@ -411,6 +479,12 @@
 
     def backward(i, _):
         b = nb - 1 - i
+        k = (g - 1) * nb + i - F_HOP * pos
+
+        @pl.when((k >= 0) & (k < FC))
+        def _():
+            first_step(k)
+
         toks = pl.ds(pl.multiple_of(b * L, L), L)
         ec, tl, dtb = ec_s[b], tl_s[b], dt_ref[:, toks]
         etot = ec[:, L - 1:L]
@@ -476,20 +550,16 @@
             dc_ref[sl, :] = dct.astype(BF16)
         lane_h = lax.broadcasted_iota(jnp.int32, (H, L), 1)
         dh_ref[...] = jnp.where(lane_h == 0, da_sum, jnp.where(lane_h == 1, dd_sum, 0.0))
-        keep(me, 0).wait()
-        for o in range(1, nd):
-            give(me, 0, o).wait_send()
-
-        @pl.when(has_second)
-        def _():
-            keep(second_of(nd, me), 1).wait()
-            for o in range(1, nd):
-                give(second_of(nd, me), 1, o).wait_send()
-
-        for k in range(KC):
-            @pl.when(me != (k if k < nd else 4 * (k - nd) + 1))
+        for k in range(FC):
+            keep(k).wait()
+
+            @pl.when(pos < ng - 1)
             def _():
-                give(k, 0, 1).wait_recv()
+                f_copy(k).wait_send()
+
+            for o in range(1, GD):
+                give(o, k).wait_send()
+                given(o, k).wait_recv()
 
 
 def carried(nd, x, dy, dt, cs, dui, rs, s_start, ds_end, b, c, par, dg, f):
@@ -505,7 +575,7 @@
         functools.partial(carried_kernel, nd),
         grid=(H // HG,),
         in_specs=[heads, heads, rows, rows, heads, rows, state, state, full((t, N)), full((t, N)), one, full((H, t)), full((H, L)),
-                  full((nb, L, L)), full((2, CR, N))],
+                  full((nb, L, L)), full((QR, N))],
         out_specs=[heads, full((H, t)), full((t, N)), full((t, N)), full((H, L)), pl.BlockSpec(memory_space=pl.ANY)],
         out_shape=[jax.ShapeDtypeStruct((H, PD, t), BF16), jax.ShapeDtypeStruct((H, t), F32), jax.ShapeDtypeStruct((t, N), BF16),
                    jax.ShapeDtypeStruct((t, N), BF16), jax.ShapeDtypeStruct((H, L), F32), jax.ShapeDtypeStruct((H * PD, N), F32)],
@@ -513,7 +583,7 @@
                         vm((HG * PD, 2 * N), BF16), vm((HG * PD, L)), vm((nb, N, L)), vm((nb, N, L)),
                         vm((nb, HG, L)), vm((nb, HG, L)), vm((nb, HG, L)), vm((nb, H, L)), vm((nb, H, L)), vm((nb, H, L)), vm((nb, H, N)),
                         vm((nb, 2 * L, N), BF16), vm((nb, 2 * L, N), BF16), vm((nb, 2 * N, L), BF16), vm((nb, N, L)),
-                        pltpu.SemaphoreType.DMA((2,)), pltpu.SemaphoreType.DMA((2, nd)), pltpu.SemaphoreType.DMA((KC,))],
+                        vm((QR, N))] + [pltpu.SemaphoreType.DMA((FC,))] * 3 + [pltpu.SemaphoreType.DMA((GD, FC))] * 2,
         compiler_params=pltpu.CompilerParams(dimension_semantics=("arbitrary",), collective_id=1, has_side_effects=True),
         cost_estimate=pl.CostEstimate(flops=5 * 10 ** 10, bytes_accessed=6 * H * PD * t, transcendentals=H * t * L),
         name="carried_backward",

time: 261 us -> 235 us (0.900)
  Pallas kernels: 245 us -> 219 us
    pallas_call x1, Pallas kernels: 137 us -> 120 us  [chain_and_blocks(): pl.pallas_call(functools.partial(chain_kernel, nd), grid=(H // HG,), in_s...]
    pallas_call x1, Pallas kernels: 19.8 us -> 15.1 us  [tile_sum(): pl.pallas_call(functools.partial(tile_sum_kernel, nd), in_specs=[vm], out...]
    pallas_call x1, Pallas kernels: 70.5 us -> 66.6 us  [carried(): pl.pallas_call(functools.partial(carried_kernel, nd), grid=(H // HG,), in...]
where the time goes in v3:
time: 235 us; the launch traced here: 234 us
  Pallas kernels  219 us (93%)
  local copies, waits for them, and re-layouts  12.4 us (5%)
    pallas_call x1, Pallas kernels, chain_and_blocks(): pl.pallas_call(functools.partial(chain_kernel, nd), grid=(H // HG,), in_s...  120 us
    pallas_call x1, Pallas kernels, carried(): pl.pallas_call(functools.partial(carried_kernel, nd), grid=(H // HG,), in...  66.6 us
    pallas_call x1, Pallas kernels, summaries(): pl.pallas_call(summary_kernel, grid=(H // HG,), in_specs=[heads, heads, f...  17.6 us
    pallas_call x1, Pallas kernels, tile_sum(): pl.pallas_call(functools.partial(tile_sum_kernel, nd), in_specs=[vm], out...  15.1 us
    unnamed x13, local copies, waits for them, and re-layouts  11.1 us

profile of v3, /device:TPU:0, one launch (start us, length us, event | category | flops | bytes accessed | tf_op | source)
XLA Modules:
  0.0 234.4 jit_solution(1265782848388919092)
XLA Ops:
  0.6 0.7 exponential_negate_fusion
  1.3 1.4 select_select_fusion.par_ref.para_ref
  2.7 17.6 %range_summaries.1 = (f32[5120,128]{1,0:T(8,128)}, f32[5120,128]{1,0:T(8,128)}, f32[80,768]{1,0:T(8,128)}, f32[80,128]{1,0:T(8,128)}) custom-call(bf16[80,64,768]{2,1,0:T(8,128)(2,1)} %bitcast.26, bf16[80,64,768]{2,1,0:T(8,128)(2,1)} %bitcast.29, f32[80,768]{1,0:T(8,128)} %bitcast.35, f32[80,128]{1,0:T(8,128)} %select_select_fusion.par_ref.para_ref, ...), custom_call_target="tpu_custom_call" | custom-call | flops 4026531840 | bytes 15728640 | tf_op jit(solution)/shard_map/range_summaries/pallas_call | solution.py:99
  20.3 120.0 %chain_and_blocks.1 = (f32[80,64,768]{2,1,0:T(8,128)}, f32[80,768]{1,0:T(8,128)}, f32[6,128,128]{2,1,0:T(8,128)}, f32[5120,128]{1,0:T(8,128)}, f32[5120,128]{1,0:T(8,128)}, /*index=5*/f32[1280,128]{1,0:T(8,128)}) custom-call(bf16[80,64,768]{2,1,0:T(8,128)(2,1)} %bitcast.27, bf16[80,64,768]{2,1,0:T(8,128)(2,1)} %bitcast.30, f32[80,768]{1,0:T(8,128)} %bitcast.36, ...), custom_call_target="tpu_custom_call" | custom-call | flops 10000000000 | bytes 10000000 | tf_op jit(solution)/shard_map/chain_and_blocks/pallas_call | solution.py:367
  140.3 66.6 %carried_backward.1 = (bf16[80,64,768]{2,1,0:T(8,128)(2,1)}, f32[80,768]{1,0:T(8,128)}, bf16[768,128]{1,0:T(8,128)(2,1)}, bf16[768,128]{1,0:T(8,128)(2,1)}, f32[80,128]{1,0:T(8,128)}, /*index=5*/f32[5120,128]{1,0:T(8,128)}) custom-call(bf16[80,64,768]{2,1,0:T(8,128)(2,1)} %bitcast.28, bf16[80,64,768]{2,1,0:T(8,128)(2,1)} %bitcast.31, f32[80,768]{1,0:T(8,128)} %bitcast.37, ...), custom_call_target="tpu_custom_call" | custom-call | flops 49999998976 | bytes 23592960 | tf_op jit(solution)/shard_map/carried_backward/pallas_call | solution.py:574
  206.9 15.1 %tile_sum.1 = f32[8,128]{1,0:T(8,128)} custom-call(f32[80,128]{1,0:T(8,128)} %get-tuple-element.38.dh_ref), custom_call_target="tpu_custom_call" | custom-call | tf_op jit(solution)/shard_map/tile_sum/pallas_call | solution.py:127
  222.0 1.3 slice_bitcast_fusion
  223.3 0.0 copy-start.1
  223.3 0.0 copy-start.3
  223.3 0.0 copy-start.2
  223.3 0.0 copy-start
  223.3 7.6 %copy.21 = bf16[1,768,80,64]{1,3,2,0:T(8,128)(2,1)} copy(bf16[1,768,80,64]{1,3,2,0:T(8,128)(2,1)} %bitcast.32) | data formatting | bytes 15728640
  230.9 0.0 copy-done.1
  230.9 0.7 copy.22
  231.6 0.0 copy-done.3
  231.6 0.7 copy.23
  232.3 0.0 copy-done.2
  232.3 0.7 copy.24
  233.0 0.0 copy-done
  233.0 1.5 copy.25
  (1 shorter events, 0.0 us)
Async XLA Ops:
  223.3 7.6 %copy-start.1 = (f32[80,768]{1,0:T(8,128)S(1)}, f32[80,768]{1,0:T(8,128)}, u32[]{:S(2)}) copy-start(f32[80,768]{1,0:T(8,128)} %get-tuple-element.34) | copy-start | bytes 737284
  223.3 8.3 %copy-start.3 = (bf16[768,128]{1,0:T(8,128)(2,1)S(1)}, bf16[768,128]{1,0:T(8,128)(2,1)}, u32[]{:S(2)}) copy-start(bf16[768,128]{1,0:T(8,128)(2,1)} %get-tuple-element.35) | copy-start | bytes 589828
  223.3 9.0 %copy-start.2 = (bf16[768,128]{1,0:T(8,128)(2,1)S(1)}, bf16[768,128]{1,0:T(8,128)(2,1)}, u32[]{:S(2)}) copy-start(bf16[768,128]{1,0:T(8,128)(2,1)} %get-tuple-element.36) | copy-start | bytes 589828
  223.3 9.7 %copy-start = (f32[5120,128]{1,0:T(8,128)S(1)}, f32[5120,128]{1,0:T(8,128)}, u32[]{:S(2)}) copy-start(f32[5120,128]{1,0:T(8,128)} %get-tuple-element.37) | copy-start | bytes 7864324

commit v4 on v3

--- a/solution.py
+++ b/solution.py
@@ -136,14 +136,15 @@
 GD = 4
 QH = H // GD
 QR = QH * PD
+F_BACK = 4
 HOP = 3
-BACK = 3
+BACK = 18
 
 
 def chain_kernel(nd, x_ref, dy_ref, dt_ref, cs_ref, b_ref, c_ref, tot_ref, s_hbm, g_hbm, s0_ref, g0_ref,
-                 dui_ref, rs_ref, dg_ref, s_end, g_end, f_ref,
-                 gram, tots, own, par, tq, tx, xin, cin, cout, bsend, brecv, dsend, into, local_sem, tot_send, tot_recv, par_send, par_recv,
-                 x_send, x_recv, c_send, c_recv, b_send, b_recv, d_send, d_recv, out_sem):
+                 dui_ref, rs_ref, dg_ref, s_end, g_end, first_ref,
+                 gram, tots, own, par, tq, tx, xin, cin, cout, bsend, brecv, dsend, into, rsum, pick, fq, fxr, local_sem, tot_send, tot_recv, par_send, par_recv,
+                 x_send, x_recv, c_send, c_recv, b_send, b_recv, d_send, d_recv, f_send, f_recv, fx_send, fx_recv, fd_send, fd_recv, out_sem):
     nb = x_ref.shape[2] // L
     ng = nd // GD
     g = pl.program_id(0)
@@ -181,6 +182,32 @@
     def d_copy(d, i, k):
         head = QH * (2 * i + core) + k
         return remote(dsend.at[d, i, rows(k)], into.at[d, rows(head)], d_send.at[d, i, k], d_recv.at[d, i, k], other_core)
+
+    def f_copy(k):
+        return remote(fq.at[rows(k)], fq.at[rows(k)], f_send.at[k], f_recv.at[k], me + 4)
+
+    def fx_copy(k):
+        return remote(fq.at[rows(k)], fxr.at[rows(k)], fx_send.at[k], fx_recv.at[k], other_chip)
+
+    def fd_copy(i, k):
+        src, head = (fq, QH * q + k) if i == 0 else (fxr, QH * oq + k)
+        return remote(src.at[rows(k)], first_ref.at[rows(head)], fd_send.at[i, k], fd_recv.at[i, k], other_core)
+
+    def f_step(k):
+        @pl.when(pos > 0)
+        def _():
+            f_copy(k).wait_recv()
+
+        @pl.when(pos < ng - 1)
+        def _():
+            f_copy(k).start()
+
+        fx_copy(k).start()
+        fd_copy(0, k).start()
+
+    def f_back(k):
+        fx_copy(k).wait_recv()
+        fd_copy(1, k).start()
 
     def decay(qq, head):
         return tots[qq, pl.ds(head, 1), :]
@@ -212,7 +239,13 @@
         e_near = jnp.exp2(decay(2 * d, head) + decay(2 * d + 1, head))
         e_far = jnp.exp2(decay(2 - 2 * d, head) + decay(3 - 2 * d, head))
         far = e_near * state + near
-        cout[d, rows(k)] = e_far * far + afar
+        out = e_far * far + afar
+        cout[d, rows(k)] = out
+
+        if d == 1:
+            @pl.when(pos == 0)
+            def _():
+                fq[rows(k)] = out
 
         @pl.when(has_next)
         def _():
@@ -237,6 +270,16 @@
             @pl.when((k >= BACK) & (k < QH + BACK))
             def _():
                 back_step(d, k - BACK)
+
+        kf = n - (HOP * (ng - 1 + pos) + 1)
+
+        @pl.when((kf >= 0) & (kf < QH))
+        def _():
+            f_step(kf)
+
+        @pl.when((kf >= F_BACK) & (kf < QH + F_BACK))
+        def _():
+            f_back(kf - F_BACK)
 
     @pl.when(g == 0)
     def _():
@@ -267,6 +310,8 @@
             sl = slice(b * L, (b + 1) * L)
             gram[b] = dot(c_ref[sl, :], b_ref[sl, :], NT)
         dg_ref[...] = jnp.zeros_like(dg_ref)
+        for j in range(2 * HG):
+            pick[j * L:(j + 1) * L, :] = (lax.broadcasted_iota(jnp.int32, (L, L), 1) == j // 2).astype(F32).astype(BF16)
         for cp in locals_[:3]:
             cp.wait()
         for o in range(1, GD):
@@ -292,7 +337,6 @@
         lax.fori_loop(0, QH, front, 0)
 
     below = lax.broadcasted_iota(jnp.int32, (L, L), 0) >= lax.broadcasted_iota(jnp.int32, (L, L), 1)
-    lane = lax.broadcasted_iota(jnp.int32, (L, L), 1)
 
     def work(b, _):
         slot(g * nb + b)
@@ -301,7 +345,6 @@
         cst = jnp.transpose(cs)
         gram_b = gram[b]
         dg = jnp.zeros((L, L), F32)
-        rs_cols = jnp.zeros((L, L), F32)
         for j in range(HG):
             xj, dyj = x_ref[j, :, toks], dy_ref[j, :, toks]
             e = jnp.exp2(jnp.where(below, jnp.broadcast_to(cst[:, j:j + 1], (L, L)) - cs[j:j + 1], NEG))
@@ -309,10 +352,9 @@
             dui_ref[j, :, toks] = dot(jnp.concatenate([dyj, dyj], axis=1), jnp.concatenate([mhi, mlo], axis=0))
             w = dot(dyj, xj, TN) * (e * dtb[j:j + 1])
             dg = dg + w
-            rs = jnp.sum(w * gram_b, axis=1, keepdims=True)
-            rs_cols = jnp.where(lane == j, jnp.broadcast_to(rs, (L, L)), rs_cols)
+            rsum[:, (2 * j) * L:(2 * j + 1) * L], rsum[:, (2 * j + 1) * L:(2 * j + 2) * L] = split(w * gram_b)
         dg_ref[b] += dg
-        rs_ref[:, toks] = jnp.transpose(rs_cols)[:HG]
+        rs_ref[:, toks] = jnp.transpose(dot(rsum[...], pick[...]))[:HG]
         return 0
 
     lax.fori_loop(0, nb, work, 0)
@@ -323,7 +365,7 @@
             slot(n)
             return 0
 
-        lax.fori_loop((H // HG) * nb, HOP * (ng - 1) + QH + BACK, rest, 0)
+        lax.fori_loop((H // HG) * nb, 2 * HOP * (ng - 1) + 1 + QH + F_BACK, rest, 0)
 
         def drain(k, _):
             for d in range(2):
@@ -336,8 +378,20 @@
 
                 for i in range(2):
                     d_copy(d, i, k).wait()
+
+            @pl.when(pos < ng - 1)
+            def _():
+                f_copy(k).wait_send()
+
+            fx_copy(k).wait_send()
+            for i in range(2):
+                fd_copy(i, k).wait()
             return 0
 
+        early = [pltpu.make_async_copy(fq, first_ref.at[rows(QH * q, QH)], out_sem.at[2]),
+                 pltpu.make_async_copy(fxr, first_ref.at[rows(QH * oq, QH)], out_sem.at[3])]
+        for out in early:
+            out.start()
         lax.fori_loop(0, QH, drain, 0)
         outs = [pltpu.make_async_copy(into.at[0], s_end, out_sem.at[0]), pltpu.make_async_copy(into.at[1], g_end, out_sem.at[1])]
         for out in outs:
@@ -347,8 +401,7 @@
         for d in range(2):
             for i in range(2):
                 par_copy(d, i).wait_send()
-        f_ref[...] = cout[1]
-        for out in outs:
+        for out in early + outs:
             out.wait()
 
 
@@ -368,69 +421,25 @@
         functools.partial(chain_kernel, nd),
         grid=(H // HG,),
         in_specs=[heads, heads, rows, rows, full((t, N)), full((t, N))] + [anywhere] * 5,
-        out_specs=[heads, rows, full((nb, L, L)), anywhere, anywhere, full((QR, N))],
-        out_shape=[jax.ShapeDtypeStruct((H, PD, t), F32), jax.ShapeDtypeStruct((H, t), F32), jax.ShapeDtypeStruct((nb, L, L), F32), state, state,
-                   jax.ShapeDtypeStruct((QR, N), F32)],
-        scratch_shapes=[pltpu.VMEM((nb, L, L), F32), pltpu.VMEM((GD, H, L), F32), whole, halves] + [quarter] * 7 + [halves, whole]
-                       + [sems(5), sems(GD), sems(GD), sems(2, 2), sems(2, 2)] + [sems(2, QH)] * 6 + [sems(2, 2, QH)] * 2 + [sems(2)],
+        out_specs=[heads, rows, full((nb, L, L)), anywhere, anywhere, anywhere],
+        out_shape=[jax.ShapeDtypeStruct((H, PD, t), F32), jax.ShapeDtypeStruct((H, t), F32), jax.ShapeDtypeStruct((nb, L, L), F32), state, state, state],
+        scratch_shapes=[pltpu.VMEM((nb, L, L), F32), pltpu.VMEM((GD, H, L), F32), whole, halves] + [quarter] * 7 + [halves, whole, pltpu.VMEM((L, 2 * HG * L), BF16), pltpu.VMEM((2 * HG * L, L), BF16),
+                           pltpu.VMEM((QR, N), F32), pltpu.VMEM((QR, N), F32)]
+                       + [sems(5), sems(GD), sems(GD), sems(2, 2), sems(2, 2)] + [sems(2, QH)] * 6 + [sems(2, 2, QH)] * 2 + [sems(QH)] * 4 + [sems(2, QH)] * 2 + [sems(4)],
         compiler_params=pltpu.CompilerParams(dimension_semantics=("arbitrary",), collective_id=0, has_side_effects=True),
         cost_estimate=pl.CostEstimate(flops=10 ** 10, bytes_accessed=10 ** 7, transcendentals=0),
         name="chain_and_blocks",
     )(x, dy, dt, cs, b, c, tot, s_loc, g_loc, s0, g0)
 
 
-FC = 5
-FR = QR // FC
-F_HOP = 5
-
-
-def carried_kernel(nd, x_ref, dy_ref, dt_ref, cs_ref, dui_ref, rs_ref, s0_ref, g1_ref, b_ref, c_ref, par_ref, dta_ref, para_ref, dg_ref, f_ref,
-                   dx_ref, ddt_ref, db_ref, dc_ref, dh_ref, first_ref,
-                   sf, gc, tu, sd, gh, us, db_acc, dc_acc, ec_s, td_s, tl_s, ddir_s, xd_s, dcs_s, kd_s, bb_ref, cc_ref, b2t_ref, ct_ref,
-                   fq, own_sem, f_send, f_recv, p_send, p_recv):
+def carried_kernel(x_ref, dy_ref, dt_ref, cs_ref, dui_ref, rs_ref, s0_ref, g1_ref, b_ref, c_ref, par_ref, dta_ref, para_ref, dg_ref,
+                   dx_ref, ddt_ref, db_ref, dc_ref, dh_ref,
+                   sf, gc, tu, sd, gh, us, db_acc, dc_acc, ec_s, td_s, tl_s, ddir_s, xd_s, dcs_s, kd_s, bb_ref, cc_ref, b2t_ref, ct_ref):
     nb = x_ref.shape[2] // L
     g = pl.program_id(0)
-    me = lax.axis_index(AXIS)
-    barrier = pltpu.get_barrier_semaphore()
-    ng = nd // GD
-    q, pos = lax.rem(me, 4), me // 4
-
-    def part(k):
-        return pl.ds(pl.multiple_of(k * FR, FR), FR)
-
-    def remote(src, dst, send, recv, to):
-        return pltpu.make_async_remote_copy(src_ref=src, dst_ref=dst, send_sem=send, recv_sem=recv, device_id=(to,), device_id_type=MESH)
-
-    def f_copy(k):
-        return remote(fq.at[part(k)], fq.at[part(k)], f_send.at[k], f_recv.at[k], me + 4)
-
-    def give(o, k):
-        return remote(fq.at[part(k)], first_ref.at[part(q * FC + k)], p_send.at[o, k], p_recv.at[o, k], 4 * pos + lax.rem(q + o, 4))
-
-    def given(o, k):
-        src = lax.rem(q + 4 - o, 4)
-        return remote(fq.at[part(k)], first_ref.at[part(src * FC + k)], p_send.at[o, k], p_recv.at[o, k], 4 * pos + src)
-
-    def keep(k):
-        return pltpu.make_async_copy(fq.at[part(k)], first_ref.at[part(q * FC + k)], own_sem.at[k])
-
-    def first_step(k):
-        @pl.when(pos > 0)
-        def _():
-            f_copy(k).wait_recv()
-
-        @pl.when(pos < ng - 1)
-        def _():
-            f_copy(k).start()
-
-        keep(k).start()
-        for o in range(1, GD):
-            give(o, k).start()
 
     @pl.when(g == 0)
     def _():
-        for o in range(1, nd):
-            pl.semaphore_signal(barrier, inc=1, device_id=(lax.rem(me + o, nd),), device_id_type=MESH)
         for b in range(nb):
             bb, cc = b_ref[b * L:(b + 1) * L, :], c_ref[b * L:(b + 1) * L, :]
             bb_ref[b] = jnp.concatenate([bb, bb], axis=0)
@@ -441,14 +450,6 @@
         db_acc[...] = jnp.zeros_like(db_acc)
         dc_acc[...] = jnp.zeros_like(dc_acc)
 
-    @pl.when(g == 1)
-    def _():
-        pl.semaphore_wait(barrier, nd - 1)
-
-        @pl.when(pos == 0)
-        def _():
-            fq[...] = f_ref[...]
-
     heads = pl.ds(pl.multiple_of(g * HG, HG), HG)
     for b in range(nb):
         sl = slice(b * L, (b + 1) * L)
@@ -479,12 +480,6 @@
 
     def backward(i, _):
         b = nb - 1 - i
-        k = (g - 1) * nb + i - F_HOP * pos
-
-        @pl.when((k >= 0) & (k < FC))
-        def _():
-            first_step(k)
-
         toks = pl.ds(pl.multiple_of(b * L, L), L)
         ec, tl, dtb = ec_s[b], tl_s[b], dt_ref[:, toks]
         etot = ec[:, L - 1:L]
@@ -513,7 +508,8 @@
             xd.append(jnp.sum(dyf * xf, axis=0, keepdims=True))
             dx_ref[j, :, toks] = (du * dtb[j:j + 1] + dyf * par_ref[j:j + 1, 1:2]).astype(BF16)
             shi, slo = split(sf[b, pr])
-            st = jnp.transpose(jnp.concatenate([shi, slo, shi, slo], axis=0))
+            st = jnp.transpose(jnp.concatenate([shi, slo], axis=0))
+            st = jnp.concatenate([st, st], axis=1)
             dhi, dlo = sd[pr, :L], sd[pr, L:]
             z = dot(st, jnp.concatenate([dhi, dhi, dlo, dlo], axis=0))
             dc = dc + z
@@ -550,19 +546,9 @@
             dc_ref[sl, :] = dct.astype(BF16)
         lane_h = lax.broadcasted_iota(jnp.int32, (H, L), 1)
         dh_ref[...] = jnp.where(lane_h == 0, da_sum, jnp.where(lane_h == 1, dd_sum, 0.0))
-        for k in range(FC):
-            keep(k).wait()
-
-            @pl.when(pos < ng - 1)
-            def _():
-                f_copy(k).wait_send()
-
-            for o in range(1, GD):
-                give(o, k).wait_send()
-                given(o, k).wait_recv()
-
-
-def carried(nd, x, dy, dt, cs, dui, rs, s_start, ds_end, b, c, par, dg, f):
+
+
+def carried(x, dy, dt, cs, dui, rs, s_start, ds_end, b, c, par, dg):
     t = x.shape[2]
     nb = t // L
     full = lambda shape: pl.BlockSpec(shape, lambda g: (0,) * len(shape))
@@ -572,22 +558,21 @@
     one = pl.BlockSpec((HG, L), lambda g: (g, 0))
     vm = lambda shape, dtype=F32: pltpu.VMEM(shape, dtype)
     return pl.pallas_call(
-        functools.partial(carried_kernel, nd),
+        carried_kernel,
         grid=(H // HG,),
         in_specs=[heads, heads, rows, rows, heads, rows, state, state, full((t, N)), full((t, N)), one, full((H, t)), full((H, L)),
-                  full((nb, L, L)), full((QR, N))],
-        out_specs=[heads, full((H, t)), full((t, N)), full((t, N)), full((H, L)), pl.BlockSpec(memory_space=pl.ANY)],
+                  full((nb, L, L))],
+        out_specs=[heads, full((H, t)), full((t, N)), full((t, N)), full((H, L))],
         out_shape=[jax.ShapeDtypeStruct((H, PD, t), BF16), jax.ShapeDtypeStruct((H, t), F32), jax.ShapeDtypeStruct((t, N), BF16),
-                   jax.ShapeDtypeStruct((t, N), BF16), jax.ShapeDtypeStruct((H, L), F32), jax.ShapeDtypeStruct((H * PD, N), F32)],
+                   jax.ShapeDtypeStruct((t, N), BF16), jax.ShapeDtypeStruct((H, L), F32)],
         scratch_shapes=[vm((nb + 1, HG * PD, N)), vm((HG * PD, N)), vm((nb, HG * PD, 2 * L), BF16), vm((HG * PD, 2 * L), BF16),
                         vm((HG * PD, 2 * N), BF16), vm((HG * PD, L)), vm((nb, N, L)), vm((nb, N, L)),
                         vm((nb, HG, L)), vm((nb, HG, L)), vm((nb, HG, L)), vm((nb, H, L)), vm((nb, H, L)), vm((nb, H, L)), vm((nb, H, N)),
-                        vm((nb, 2 * L, N), BF16), vm((nb, 2 * L, N), BF16), vm((nb, 2 * N, L), BF16), vm((nb, N, L)),
-                        vm((QR, N))] + [pltpu.SemaphoreType.DMA((FC,))] * 3 + [pltpu.SemaphoreType.DMA((GD, FC))] * 2,
-        compiler_params=pltpu.CompilerParams(dimension_semantics=("arbitrary",), collective_id=1, has_side_effects=True),
+                        vm((nb, 2 * L, N), BF16), vm((nb, 2 * L, N), BF16), vm((nb, 2 * N, L), BF16), vm((nb, N, L))],
+        compiler_params=pltpu.CompilerParams(dimension_semantics=("arbitrary",)),
         cost_estimate=pl.CostEstimate(flops=5 * 10 ** 10, bytes_accessed=6 * H * PD * t, transcendentals=H * t * L),
         name="carried_backward",
-    )(x, dy, dt, cs, dui, rs, s_start, ds_end, b, c, par, dt, par, dg, f)
+    )(x, dy, dt, cs, dui, rs, s_start, ds_end, b, c, par, dt, par, dg)
 
 
 def solution(mesh):
@@ -603,8 +588,8 @@
         par = jnp.where(col == 0, -jnp.exp(a_log)[:, None], jnp.where(col == 1, d_skip[:, None], 0.0))
         s_loc, g_loc, cs, tot = summaries(x, dy, dt, par, b, c)
         s0, g0 = s_init.reshape(H * PD, N), ds_last.reshape(H * PD, N)
-        dui, rs, dg, s_start, ds_end, f = chain_and_blocks(nd, x, dy, dt, cs, b, c, tot, s_loc, g_loc, s0, g0)
-        dx, ddt, db, dc, dh, first = carried(nd, x, dy, dt, cs, dui, rs, s_start, ds_end, b, c, par, dg, f)
+        dui, rs, dg, s_start, ds_end, first = chain_and_blocks(nd, x, dy, dt, cs, b, c, tot, s_loc, g_loc, s0, g0)
+        dx, ddt, db, dc, dh = carried(x, dy, dt, cs, dui, rs, s_start, ds_end, b, c, par, dg)
         dh = tile_sum(nd, dh)
         return (jnp.transpose(dx, (2, 0, 1))[None], jnp.transpose(ddt)[None], db[None], dc[None], first.reshape(1, H, PD, N), dh[0, :H], dh[1, :H])
 

time: 235 us -> 214 us (0.911)
  Pallas kernels: 219 us -> 208 us
  local copies, waits for them, and re-layouts: 12.4 us -> 2.77 us
    unnamed x13 -> x3, local copies, waits for them, and re-layouts: 11.1 us -> 1.5 us
    pallas_call x1, Pallas kernels: 120 us -> 111 us  [chain_and_blocks(): pl.pallas_call(functools.partial(chain_kernel, nd), grid=(H // HG,), in_s...]
    pallas_call x1, Pallas kernels: 66.6 us -> 63.5 us  [carried(): pl.pallas_call(carried_kernel, grid=(H // HG,), in_specs=[heads, heads, r...]
where the time goes in v4:
time: 214 us; the launch traced here: 213 us
  Pallas kernels  208 us (97%)
  local copies, waits for them, and re-layouts  2.77 us (1%)
    pallas_call x1, Pallas kernels, chain_and_blocks(): pl.pallas_call(functools.partial(chain_kernel, nd), grid=(H // HG,), in_s...  111 us
    pallas_call x1, Pallas kernels, carried(): pl.pallas_call(carried_kernel, grid=(H // HG,), in_specs=[heads, heads, r...  63.5 us
    pallas_call x1, Pallas kernels, summaries(): pl.pallas_call(summary_kernel, grid=(H // HG,), in_specs=[heads, heads, f...  17.6 us
    pallas_call x1, Pallas kernels, tile_sum(): pl.pallas_call(functools.partial(tile_sum_kernel, nd), in_specs=[vm], out...  15.6 us

profile of v4, /device:TPU:0, one launch (start us, length us, event | category | flops | bytes accessed | tf_op | source)
XLA Modules:
  0.0 213.4 jit_solution(8165071285064013432)
XLA Ops:
  0.6 0.7 exponential_negate_fusion
  1.3 1.4 select_select_fusion.par_ref.para_ref
  2.7 17.6 %range_summaries.1 = (f32[5120,128]{1,0:T(8,128)}, f32[5120,128]{1,0:T(8,128)}, f32[80,768]{1,0:T(8,128)}, f32[80,128]{1,0:T(8,128)}) custom-call(bf16[80,64,768]{2,1,0:T(8,128)(2,1)} %bitcast.26, bf16[80,64,768]{2,1,0:T(8,128)(2,1)} %bitcast.29, f32[80,768]{1,0:T(8,128)} %bitcast.33, f32[80,128]{1,0:T(8,128)} %select_select_fusion.par_ref.para_ref, ...), custom_call_target="tpu_custom_call" | custom-call | flops 4026531840 | bytes 15728640 | tf_op jit(solution)/shard_map/range_summaries/pallas_call | solution.py:99
  20.3 111.2 %chain_and_blocks.1 = (f32[80,64,768]{2,1,0:T(8,128)}, f32[80,768]{1,0:T(8,128)}, f32[6,128,128]{2,1,0:T(8,128)}, f32[5120,128]{1,0:T(8,128)}, f32[5120,128]{1,0:T(8,128)}, /*index=5*/f32[5120,128]{1,0:T(8,128)}) custom-call(bf16[80,64,768]{2,1,0:T(8,128)(2,1)} %bitcast.27, bf16[80,64,768]{2,1,0:T(8,128)(2,1)} %bitcast.30, f32[80,768]{1,0:T(8,128)} %bitcast.34, ...), custom_call_target="tpu_custom_call" | custom-call | flops 10000000000 | bytes 10000000 | tf_op jit(solution)/shard_map/chain_and_blocks/pallas_call | solution.py:420
  131.4 0.0 copy-start
  131.5 63.5 %carried_backward.1 = (bf16[80,64,768]{2,1,0:T(8,128)(2,1)}, f32[80,768]{1,0:T(8,128)}, bf16[768,128]{1,0:T(8,128)(2,1)}, bf16[768,128]{1,0:T(8,128)(2,1)}, f32[80,128]{1,0:T(8,128)}) custom-call(bf16[80,64,768]{2,1,0:T(8,128)(2,1)} %bitcast.28, bf16[80,64,768]{2,1,0:T(8,128)(2,1)} %bitcast.31, f32[80,768]{1,0:T(8,128)} %bitcast.35, ...), custom_call_target="tpu_custom_call" | custom-call | flops 49999998976 | bytes 23592960 | tf_op jit(solution)/shard_map/carried_backward/pallas_call | solution.py:560
  195.0 15.6 %tile_sum.1 = f32[8,128]{1,0:T(8,128)} custom-call(f32[80,128]{1,0:T(8,128)} %get-tuple-element.36.dh_ref), custom_call_target="tpu_custom_call" | custom-call | tf_op jit(solution)/shard_map/tile_sum/pallas_call | solution.py:127
  210.6 1.3 slice_bitcast_fusion
  211.9 0.0 copy-done
  211.9 1.5 copy.17
  (1 shorter events, 0.0 us)
Async XLA Ops:
  131.4 80.4 %copy-start = (f32[5120,128]{1,0:T(8,128)S(1)}, f32[5120,128]{1,0:T(8,128)}, u32[]{:S(2)}) copy-start(f32[5120,128]{1,0:T(8,128)} %get-tuple-element.35) | copy-start | bytes 7864324

commit v5 on v4

--- a/solution.py
+++ b/solution.py
@@ -136,9 +136,9 @@
 GD = 4
 QH = H // GD
 QR = QH * PD
-F_BACK = 4
+F_BACK = 8
 HOP = 3
-BACK = 18
+BACK = 20
 
 
 def chain_kernel(nd, x_ref, dy_ref, dt_ref, cs_ref, b_ref, c_ref, tot_ref, s_hbm, g_hbm, s0_ref, g0_ref,
@@ -183,8 +183,10 @@
         head = QH * (2 * i + core) + k
         return remote(dsend.at[d, i, rows(k)], into.at[d, rows(head)], d_send.at[d, i, k], d_recv.at[d, i, k], other_core)
 
-    def f_copy(k):
-        return remote(fq.at[rows(k)], fq.at[rows(k)], f_send.at[k], f_recv.at[k], me + 4)
+    f_sends = ((lax.rem(pos, 2) == 0) & (pos < ng - 2), lax.rem(pos, 2) == 0)
+
+    def f_copy(way, k):
+        return remote(fq.at[rows(k)], fq.at[rows(k)], f_send.at[way, k], f_recv.at[k], me + (8 - 4 * way))
 
     def fx_copy(k):
         return remote(fq.at[rows(k)], fxr.at[rows(k)], fx_send.at[k], fx_recv.at[k], other_chip)
@@ -196,11 +198,12 @@
     def f_step(k):
         @pl.when(pos > 0)
         def _():
-            f_copy(k).wait_recv()
-
-        @pl.when(pos < ng - 1)
-        def _():
-            f_copy(k).start()
+            f_copy(0, k).wait_recv()
+
+        for way in range(2):
+            @pl.when(f_sends[way])
+            def _():
+                f_copy(way, k).start()
 
         fx_copy(k).start()
         fd_copy(0, k).start()
@@ -271,7 +274,7 @@
             def _():
                 back_step(d, k - BACK)
 
-        kf = n - (HOP * (ng - 1 + pos) + 1)
+        kf = n - (HOP * (ng - 1 + pos // 2 + lax.rem(pos, 2)) + 1)
 
         @pl.when((kf >= 0) & (kf < QH))
         def _():
@@ -327,14 +330,17 @@
             e_far = jnp.exp2(decay(2 * chip + 1 - d, head))
             return e_far * jnp.where(mine_near, mine, his) + jnp.where(mine_near, his, mine)
 
-        def front(k, _):
+        def front(turn, k, _):
             for d in range(2):
-                tx[d, rows(k)] = combine(d, 1 - chip, k)
-                x_copy(d, k).start()
-                tq[d, rows(k)] = combine(d, chip, k)
+                @pl.when((turn == d) == (pos < ng // 2))
+                def _():
+                    tx[d, rows(k)] = combine(d, 1 - chip, k)
+                    x_copy(d, k).start()
+                    tq[d, rows(k)] = combine(d, chip, k)
             return 0
 
-        lax.fori_loop(0, QH, front, 0)
+        for turn in (0, 1):
+            lax.fori_loop(0, QH, functools.partial(front, turn), 0)
 
     below = lax.broadcasted_iota(jnp.int32, (L, L), 0) >= lax.broadcasted_iota(jnp.int32, (L, L), 1)
 
@@ -365,7 +371,7 @@
             slot(n)
             return 0
 
-        lax.fori_loop((H // HG) * nb, 2 * HOP * (ng - 1) + 1 + QH + F_BACK, rest, 0)
+        lax.fori_loop((H // HG) * nb, max(HOP * (ng - 1) + BACK, HOP * (ng - 1 + ng // 2) + 1 + F_BACK) + QH, rest, 0)
 
         def drain(k, _):
             for d in range(2):
@@ -379,9 +385,10 @@
                 for i in range(2):
                     d_copy(d, i, k).wait()
 
-            @pl.when(pos < ng - 1)
-            def _():
-                f_copy(k).wait_send()
+            for way in range(2):
+                @pl.when(f_sends[way])
+                def _():
+                    f_copy(way, k).wait_send()
 
             fx_copy(k).wait_send()
             for i in range(2):
@@ -425,7 +432,7 @@
         out_shape=[jax.ShapeDtypeStruct((H, PD, t), F32), jax.ShapeDtypeStruct((H, t), F32), jax.ShapeDtypeStruct((nb, L, L), F32), state, state, state],
         scratch_shapes=[pltpu.VMEM((nb, L, L), F32), pltpu.VMEM((GD, H, L), F32), whole, halves] + [quarter] * 7 + [halves, whole, pltpu.VMEM((L, 2 * HG * L), BF16), pltpu.VMEM((2 * HG * L, L), BF16),
                            pltpu.VMEM((QR, N), F32), pltpu.VMEM((QR, N), F32)]
-                       + [sems(5), sems(GD), sems(GD), sems(2, 2), sems(2, 2)] + [sems(2, QH)] * 6 + [sems(2, 2, QH)] * 2 + [sems(QH)] * 4 + [sems(2, QH)] * 2 + [sems(4)],
+                       + [sems(5), sems(GD), sems(GD), sems(2, 2), sems(2, 2)] + [sems(2, QH)] * 6 + [sems(2, 2, QH)] * 2 + [sems(2, QH)] + [sems(QH)] * 3 + [sems(2, QH)] * 2 + [sems(4)],
         compiler_params=pltpu.CompilerParams(dimension_semantics=("arbitrary",), collective_id=0, has_side_effects=True),
         cost_estimate=pl.CostEstimate(flops=10 ** 10, bytes_accessed=10 ** 7, transcendentals=0),
         name="chain_and_blocks",
@@ -496,7 +503,8 @@
             sd[pr, L:] = lo
         kd_s[b, heads] = jnp.concatenate(kd, axis=0)
         us[...] = dot(gh[...], b2t_ref[b])
-        db_acc[b] += (dot(gh[:, :L], tu[b, :, :L], TN) + dot(gh[:, L:], tu[b, :, :L], TN)) + dot(gh[:, :L], tu[b, :, L:], TN)
+        wide = dot(gh[...], tu[b], TN)
+        db_acc[b] += (wide[:N, :L] + wide[:N, L:]) + (wide[N:, :L] + wide[N:, L:])
         ct = ct_ref[b]
         dc = jnp.zeros((N, L), F32)
         ddir, xd, inter = [], [], []

time: 214 us -> 201 us (0.939)
  Pallas kernels: 208 us -> 195 us
    pallas_call x1, Pallas kernels: 15.6 us -> 9.5 us  [tile_sum(): pl.pallas_call(functools.partial(tile_sum_kernel, nd), in_specs=[vm], out...]
    pallas_call x1, Pallas kernels: 63.5 us -> 59.7 us  [carried(): pl.pallas_call(carried_kernel, grid=(H // HG,), in_specs=[heads, heads, r...]
    pallas_call x1, Pallas kernels: 111 us -> 108 us  [chain_and_blocks(): pl.pallas_call(functools.partial(chain_kernel, nd), grid=(H // HG,), in_s...]
where the time goes in v5:
time: 201 us; the launch traced here: 200 us
  Pallas kernels  195 us (97%)
  local copies, waits for them, and re-layouts  2.77 us (1%)
  other arithmetic  2.03 us (1%)
    pallas_call x1, Pallas kernels, chain_and_blocks(): pl.pallas_call(functools.partial(chain_kernel, nd), grid=(H // HG,), in_s...  108 us
    pallas_call x1, Pallas kernels, carried(): pl.pallas_call(carried_kernel, grid=(H // HG,), in_specs=[heads, heads, r...  59.7 us
    pallas_call x1, Pallas kernels, summaries(): pl.pallas_call(summary_kernel, grid=(H // HG,), in_specs=[heads, heads, f...  17.6 us
    pallas_call x1, Pallas kernels, tile_sum(): pl.pallas_call(functools.partial(tile_sum_kernel, nd), in_specs=[vm], out...  9.5 us

profile of v5, /device:TPU:0, one launch (start us, length us, event | category | flops | bytes accessed | tf_op | source)
XLA Modules:
  0.0 200.2 jit_solution(1989903380891365117)
XLA Ops:
  0.6 0.7 exponential_negate_fusion
  1.3 1.4 select_select_fusion.par_ref.para_ref
  2.7 17.6 %range_summaries.1 = (f32[5120,128]{1,0:T(8,128)}, f32[5120,128]{1,0:T(8,128)}, f32[80,768]{1,0:T(8,128)}, f32[80,128]{1,0:T(8,128)}) custom-call(bf16[80,64,768]{2,1,0:T(8,128)(2,1)} %bitcast.26, bf16[80,64,768]{2,1,0:T(8,128)(2,1)} %bitcast.29, f32[80,768]{1,0:T(8,128)} %bitcast.33, f32[80,128]{1,0:T(8,128)} %select_select_fusion.par_ref.para_ref, ...), custom_call_target="tpu_custom_call" | custom-call | flops 4026531840 | bytes 15728640 | tf_op jit(solution)/shard_map/range_summaries/pallas_call | solution.py:99
  20.3 107.9 %chain_and_blocks.1 = (f32[80,64,768]{2,1,0:T(8,128)}, f32[80,768]{1,0:T(8,128)}, f32[6,128,128]{2,1,0:T(8,128)}, f32[5120,128]{1,0:T(8,128)}, f32[5120,128]{1,0:T(8,128)}, /*index=5*/f32[5120,128]{1,0:T(8,128)}) custom-call(bf16[80,64,768]{2,1,0:T(8,128)(2,1)} %bitcast.27, bf16[80,64,768]{2,1,0:T(8,128)(2,1)} %bitcast.30, f32[80,768]{1,0:T(8,128)} %bitcast.34, ...), custom_call_target="tpu_custom_call" | custom-call | flops 10000000000 | bytes 10000000 | tf_op jit(solution)/shard_map/chain_and_blocks/pallas_call | solution.py:427
  128.2 0.0 copy-start
  128.2 59.7 %carried_backward.1 = (bf16[80,64,768]{2,1,0:T(8,128)(2,1)}, f32[80,768]{1,0:T(8,128)}, bf16[768,128]{1,0:T(8,128)(2,1)}, bf16[768,128]{1,0:T(8,128)(2,1)}, f32[80,128]{1,0:T(8,128)}) custom-call(bf16[80,64,768]{2,1,0:T(8,128)(2,1)} %bitcast.28, bf16[80,64,768]{2,1,0:T(8,128)(2,1)} %bitcast.31, f32[80,768]{1,0:T(8,128)} %bitcast.35, ...), custom_call_target="tpu_custom_call" | custom-call | flops 49999998976 | bytes 23592960 | tf_op jit(solution)/shard_map/carried_backward/pallas_call | solution.py:568
  188.0 9.5 %tile_sum.1 = f32[8,128]{1,0:T(8,128)} custom-call(f32[80,128]{1,0:T(8,128)} %get-tuple-element.36.dh_ref), custom_call_target="tpu_custom_call" | custom-call | tf_op jit(solution)/shard_map/tile_sum/pallas_call | solution.py:127
  197.5 1.3 slice_bitcast_fusion
  198.7 0.0 copy-done
  198.7 1.5 copy.17
  (1 shorter events, 0.0 us)
Async XLA Ops:
  128.2 70.5 %copy-start = (f32[5120,128]{1,0:T(8,128)S(1)}, f32[5120,128]{1,0:T(8,128)}, u32[]{:S(2)}) copy-start(f32[5120,128]{1,0:T(8,128)} %get-tuple-element.35) | copy-start | bytes 7864324

commit v6 on v5

--- a/solution.py
+++ b/solution.py
@@ -136,7 +136,8 @@
 GD = 4
 QH = H // GD
 QR = QH * PD
-F_BACK = 8
+F_HOP = 5
+F_BACK = 12
 HOP = 3
 BACK = 20
 
@@ -274,7 +275,7 @@
             def _():
                 back_step(d, k - BACK)
 
-        kf = n - (HOP * (ng - 1 + pos // 2 + lax.rem(pos, 2)) + 1)
+        kf = n - (HOP * (ng - 1) + F_HOP * (pos // 2 + lax.rem(pos, 2)) + 1)
 
         @pl.when((kf >= 0) & (kf < QH))
         def _():
@@ -371,7 +372,7 @@
             slot(n)
             return 0
 
-        lax.fori_loop((H // HG) * nb, max(HOP * (ng - 1) + BACK, HOP * (ng - 1 + ng // 2) + 1 + F_BACK) + QH, rest, 0)
+        lax.fori_loop((H // HG) * nb, max(HOP * (ng - 1) + BACK, HOP * (ng - 1) + F_HOP * (ng // 2) + 1 + F_BACK) + QH, rest, 0)
 
         def drain(k, _):
             for d in range(2):

time: 201 us -> 198 us (0.985)
  Pallas kernels: 195 us -> 192 us
    pallas_call x1, Pallas kernels: 108 us -> 105 us  [chain_and_blocks(): pl.pallas_call(functools.partial(chain_kernel, nd), grid=(H // HG,), in_s...]
where the time goes in v6:
time: 198 us; the launch traced here: 197 us
  Pallas kernels  192 us (97%)
  local copies, waits for them, and re-layouts  2.77 us (1%)
  other arithmetic  2.03 us (1%)
    pallas_call x1, Pallas kernels, chain_and_blocks(): pl.pallas_call(functools.partial(chain_kernel, nd), grid=(H // HG,), in_s...  105 us
    pallas_call x1, Pallas kernels, carried(): pl.pallas_call(carried_kernel, grid=(H // HG,), in_specs=[heads, heads, r...  59.7 us
    pallas_call x1, Pallas kernels, summaries(): pl.pallas_call(summary_kernel, grid=(H // HG,), in_specs=[heads, heads, f...  17.6 us
    pallas_call x1, Pallas kernels, tile_sum(): pl.pallas_call(functools.partial(tile_sum_kernel, nd), in_specs=[vm], out...  9.5 us

profile of v6, /device:TPU:0, one launch (start us, length us, event | category | flops | bytes accessed | tf_op | source)
XLA Modules:
  0.0 197.3 jit_solution(9129859116129390893)
XLA Ops:
  0.6 0.7 exponential_negate_fusion
  1.3 1.4 select_select_fusion.par_ref.para_ref
  2.7 17.6 %range_summaries.1 = (f32[5120,128]{1,0:T(8,128)}, f32[5120,128]{1,0:T(8,128)}, f32[80,768]{1,0:T(8,128)}, f32[80,128]{1,0:T(8,128)}) custom-call(bf16[80,64,768]{2,1,0:T(8,128)(2,1)} %bitcast.26, bf16[80,64,768]{2,1,0:T(8,128)(2,1)} %bitcast.29, f32[80,768]{1,0:T(8,128)} %bitcast.33, f32[80,128]{1,0:T(8,128)} %select_select_fusion.par_ref.para_ref, ...), custom_call_target="tpu_custom_call" | custom-call | flops 4026531840 | bytes 15728640 | tf_op jit(solution)/shard_map/range_summaries/pallas_call | solution.py:99
  20.3 105.0 %chain_and_blocks.1 = (f32[80,64,768]{2,1,0:T(8,128)}, f32[80,768]{1,0:T(8,128)}, f32[6,128,128]{2,1,0:T(8,128)}, f32[5120,128]{1,0:T(8,128)}, f32[5120,128]{1,0:T(8,128)}, /*index=5*/f32[5120,128]{1,0:T(8,128)}) custom-call(bf16[80,64,768]{2,1,0:T(8,128)(2,1)} %bitcast.27, bf16[80,64,768]{2,1,0:T(8,128)(2,1)} %bitcast.30, f32[80,768]{1,0:T(8,128)} %bitcast.34, ...), custom_call_target="tpu_custom_call" | custom-call | flops 10000000000 | bytes 10000000 | tf_op jit(solution)/shard_map/chain_and_blocks/pallas_call | solution.py:428
  125.3 0.0 copy-start
  125.3 59.7 %carried_backward.1 = (bf16[80,64,768]{2,1,0:T(8,128)(2,1)}, f32[80,768]{1,0:T(8,128)}, bf16[768,128]{1,0:T(8,128)(2,1)}, bf16[768,128]{1,0:T(8,128)(2,1)}, f32[80,128]{1,0:T(8,128)}) custom-call(bf16[80,64,768]{2,1,0:T(8,128)(2,1)} %bitcast.28, bf16[80,64,768]{2,1,0:T(8,128)(2,1)} %bitcast.31, f32[80,768]{1,0:T(8,128)} %bitcast.35, ...), custom_call_target="tpu_custom_call" | custom-call | flops 49999998976 | bytes 23592960 | tf_op jit(solution)/shard_map/carried_backward/pallas_call | solution.py:569
  185.0 9.5 %tile_sum.1 = f32[8,128]{1,0:T(8,128)} custom-call(f32[80,128]{1,0:T(8,128)} %get-tuple-element.36.dh_ref), custom_call_target="tpu_custom_call" | custom-call | tf_op jit(solution)/shard_map/tile_sum/pallas_call | solution.py:127
  194.5 1.3 slice_bitcast_fusion
  195.8 0.0 copy-done
  195.8 1.5 copy.17
  (1 shorter events, 0.0 us)
Async XLA Ops:
  125.3 70.5 %copy-start = (f32[5120,128]{1,0:T(8,128)S(1)}, f32[5120,128]{1,0:T(8,128)}, u32[]{:S(2)}) copy-start(f32[5120,128]{1,0:T(8,128)} %get-tuple-element.35) | copy-start | bytes 7864324
